TPU v7x, 256 devices: a whole 4x4x8 slice. The times are simulated.
256 devices in a mesh: seq: 32 (over z, x), head: 8 (over y, core).
Axes of the slice: x: 4, y: 4, z: 8, core: 2. Of those that a mesh axis runs over, the one named last changes fastest.
Arguments:
- queries: bfloat16 [8192, 1024], P('seq', 'head'), may hold values from -16 to 16
- keys: bfloat16 [8192, 1024], P(('seq', 'head')), may hold values from -16 to 16
- values: bfloat16 [8192, 1024], P(('seq', 'head')), may hold values from -6 to 6
- out_grad: bfloat16 [8192, 1024], P('seq', 'head'), may hold values from -6 to 6
Outputs:
- attended: bfloat16 [8192, 1024], P('seq', 'head')
- query_grad: float32 [8192, 1024], P('seq', 'head')
- key_grad: float32 [8192, 1024], P('seq', 'head')
- value_grad: float32 [8192, 1024], P('seq', 'head')
All inputs are finite; a program needn't handle non-finite values.
Results may differ from a plain program's by a relative error of at most 0.0095.
Values may be sent and summed in bfloat16 or wider, within the bound.
No kernel may reach another device: no remote copies, remote signals or barrier semaphores. Data moves between devices by JAX's collectives and lax.ppermute only.
A program may use at most 64 MiB of HBM per device.

v0:
```python
import functools
import math

import jax
import jax.numpy as jnp
from jax import lax
from jax.experimental import pallas as pl
from jax.experimental.pallas import tpu as pltpu
from jax.sharding import Mesh
from jax.sharding import PartitionSpec as P

Z = ("zj", "zp")
SEQ = (*Z, "x")
VMEM = 24 << 20
PIECES = (3, 2, 2)
LOW = -1e30
F32 = jnp.float32
BF16 = jnp.bfloat16
NT = (((1,), (1,)), ((), ()))
TN = (((0,), (0,)), ((), ()))
NN = (((1,), (0,)), ((), ()))


def dot(a, b, dims):
    return lax.dot_general(a, b, dims, preferred_element_type=F32)


def allowed_pairs(rows, key_block, query_block):
    key_pos = lax.broadcasted_iota(jnp.int32, (rows, rows), 0) + key_block * rows
    query_pos = lax.broadcasted_iota(jnp.int32, (rows, rows), 1) + query_block * rows
    return key_pos <= query_pos


def prepare_kernel(nh, q_ref, g_ref, k_ref, v_ref, own_ref, mixed_ref, kv_ref, sems):
    width = q_ref.shape[1]
    moves = [
        pltpu.make_async_copy(k_ref, kv_ref.at[0], sems.at[0]),
        pltpu.make_async_copy(v_ref, kv_ref.at[1], sems.at[1]),
        pltpu.make_async_copy(q_ref, own_ref.at[:, :width], sems.at[2]),
        pltpu.make_async_copy(g_ref, own_ref.at[:, width:], sems.at[3]),
    ]
    for move in moves:
        move.start()
    for part in range(2):
        moves[part].wait()
        for at in range(mixed_ref.shape[0]):
            cols = slice(at % nh * width, (at % nh + 1) * width)
            mixed_ref[at, :, part * width : (part + 1) * width] = kv_ref[part, :, cols]
    moves[2].wait()
    moves[3].wait()


def pieces(value, count):
    out = []
    for _ in range(count):
        out.append(value.astype(BF16))
        value = value - out[-1].astype(F32)
    return out


def gather_blocks(q_refs, query_ref, grad_ref):
    rows, width = q_refs[0].shape[0], q_refs[0].shape[1] // 2
    count = len(q_refs) // 2
    for at, ref in enumerate(q_refs):
        side, r = divmod(at, count)
        query_ref[side, r * rows : (r + 1) * rows, :] = ref[:, :width]
        grad_ref[side, r * rows : (r + 1) * rows, :] = ref[:, width:]


def each_unit(where_ref, unit):
    own, other = where_ref[0], where_ref[1]

    @pl.loop(0, own)
    def _(j):
        unit(j, 0, j, False)

    unit(own, 0, own, True)

    @pl.loop(0, other)
    def _(j):
        unit(own + 1 + j, 1, j, False)


def folded(value, op):
    return op(value.reshape(value.shape[0] // 8, 8, value.shape[1]), axis=0)


def forward_kernel(rate, nx, where_ref, *refs):
    q_refs, (kv_ref, send_ref, s_ref), refs = refs[: 2 * nx], refs[2 * nx : 2 * nx + 3], refs[2 * nx + 3 :]
    stat_ref, o_ref, m_ref, l_ref, query_ref, grad_ref = refs
    x, even = where_ref[2], where_ref[3]
    rows, width = kv_ref.shape[1], kv_ref.shape[2] // 2
    gather_blocks(q_refs, query_ref, grad_ref)
    m_ref[...] = jnp.full_like(m_ref, LOW)
    l_ref[...] = jnp.zeros_like(l_ref)
    o_ref[...] = jnp.zeros_like(o_ref)

    def score(u, side, j, masked):
        s = dot(kv_ref[j, :, :width], query_ref[side], NT)
        if masked:
            oks = [allowed_pairs(rows, x, lax.rem(x - r + nx, nx)) for r in range(nx)]
            s = jnp.where(jnp.concatenate(oks, axis=1), s, LOW)
        s_ref[u] = s
        m_ref[side] = jnp.maximum(m_ref[side], folded(s, jnp.max))

    def weigh(u, side, j, masked):
        p = jnp.exp2((s_ref[u] - m_ref[side, 0:1, :]) * rate)
        l_ref[side] += folded(p, jnp.sum)
        o_ref[side] += dot(kv_ref[j, :, width:], p.astype(BF16), TN)

    each_unit(where_ref, score)
    for side in range(2):
        m_ref[side, 0:1, :] = jnp.maximum(
            jnp.max(m_ref[side], axis=0, keepdims=True), LOW / 2
        )
    each_unit(where_ref, weigh)
    for side in range(2):
        total = jnp.sum(l_ref[side], axis=0, keepdims=True)
        grads = jnp.transpose(grad_ref[side].astype(F32))
        inner = jnp.sum(grads * o_ref[side], axis=0, keepdims=True)
        for r in range(nx):
            cols = slice(r * rows, (r + 1) * rows)
            to = (side ^ even) * nx + lax.rem(x - r + nx, nx)
            row = pl.ds(to, 1)
            stat_ref[0, row, :] = m_ref[side, 0:1, cols] * rate
            stat_ref[1, row, :] = total[:, cols]
            stat_ref[2, row, :] = inner[:, cols]
            send_ref[to, :width, :] = o_ref[side, :, cols].astype(BF16)
    base = width
    for q, count in enumerate(PIECES):
        for piece in pieces(stat_ref[q], count):
            for to in range(2 * nx):
                send_ref[to, base : base + 2 * nx, :] = piece
            base += 2 * nx


def read_stats(got_ref, stat_ref, base, n):
    for q, count in enumerate(PIECES):
        for i in range(n):
            stat_ref[i, q] = sum(
                got_ref[i, base + c * n : base + (c + 1) * n, :].astype(F32) for c in range(count)
            )
        base += count * n


def backward_kernel(rate, scaling, nx, where_ref, *refs):
    n = 2 * nx
    q_refs, (kv_ref, got_ref, s_ref), refs = refs[:n], refs[n : n + 3], refs[n + 3 :]
    nj = kv_ref.shape[0]
    out_refs, key_refs, refs = refs[:nx], refs[nx : nx + nj], refs[nx + nj :]
    dq_ref, norm_ref, delta_ref, acc_ref, stat_ref, query_ref, grad_ref = refs
    x, even = where_ref[2], where_ref[3]
    rows, width = kv_ref.shape[1], kv_ref.shape[2] // 2
    read_stats(got_ref, stat_ref, width, n)
    gather_blocks(q_refs, query_ref, grad_ref)
    dq_ref[...] = jnp.zeros_like(dq_ref)
    acc_ref[...] = jnp.zeros_like(acc_ref)
    top = functools.reduce(jnp.maximum, [stat_ref[i, 0] for i in range(n)])
    shares = [jnp.exp2(stat_ref[i, 0] - top) for i in range(n)]
    total = sum(stat_ref[i, 1] * w for i, w in enumerate(shares))
    delta = sum(stat_ref[i, 2] * w for i, w in enumerate(shares))
    stat_ref[0, 0] = top + jnp.log2(total)
    stat_ref[0, 1] = delta / total
    for at in range(n):
        side, r = divmod(at, nx)
        cols = slice(r * rows, (r + 1) * rows)
        row = pl.ds((side ^ even) * nx + lax.rem(x - r + nx, nx), 1)
        norm_ref[side, :, cols] = stat_ref[0, 0, row, :]
        delta_ref[side, :, cols] = stat_ref[0, 1, row, :]

    def unit(u, side, j, masked):
        k, v = kv_ref[j, :, :width], kv_ref[j, :, width:]
        p = jnp.exp2(s_ref[u] * rate - norm_ref[side])
        ds = (p * (dot(v, grad_ref[side], NT) - delta_ref[side])).astype(BF16)
        acc_ref[j, :, width:] += dot(p.astype(BF16), grad_ref[side], NN)
        acc_ref[j, :, :width] += dot(ds, query_ref[side], NN)
        dq_ref[side] += dot(k, ds, TN)

    each_unit(where_ref, unit)
    for step in range(nj):
        to = lax.rem(where_ref[0] + step, nj)
        key_refs[step][:, :width] = (acc_ref[to, :, :width] * scaling).astype(BF16)
        key_refs[step][:, width:] = acc_ref[to, :, width:].astype(BF16)
    for at in range(n):
        side, r = divmod(at, nx)
        out_refs[r][:, side * rows : (side + 1) * rows] = (
            dq_ref[side, :, r * rows : (r + 1) * rows] * scaling
        ).astype(BF16)


def mix_kernel(nx, where_ref, got_ref, out_ref, stat_ref):
    n = 2 * nx
    rows, width = out_ref.shape
    read_stats(got_ref, stat_ref, width, n)
    row = pl.ds(where_ref[3] * nx + where_ref[2], 1)
    maxima = [stat_ref[i, 0, row, :] for i in range(n)]
    top = functools.reduce(jnp.maximum, maxima)
    shares = [jnp.exp2(m - top) for m in maxima]
    total = sum(stat_ref[i, 1, row, :] * w for i, w in enumerate(shares))
    mixed = jnp.zeros((width, rows), F32)
    for i, share in enumerate(shares):
        mixed = mixed + share * got_ref[i, :width, :]
    out_ref[...] = jnp.transpose(mixed / total).astype(BF16)


def final_kernel(nx, nj, *refs):
    part_refs, back_ref, key_refs, outs = refs[:nx], refs[nx], refs[nx + 1 : -3], refs[-3:]
    rows, width = outs[0].shape
    dq = back_ref[...].astype(F32)
    for part in part_refs:
        dq = dq + part[:, :rows]
    outs[0][...] = jnp.transpose(dq)
    total = key_refs[0][...].astype(F32)
    for j in range(1, nj):
        total = total + key_refs[j][...]
    outs[1][...] = total[:, :width]
    outs[2][...] = total[:, width:]


def shifted(value, axis, count, step):
    return lax.ppermute(value, axis, [(i, (i + step) % count) for i in range(count)])


def swapped(value, count):
    pairs = [(i, (i + 1) % count) for i in range(1, count, 2)]
    return lax.ppermute(value, Z, pairs + [(j, i) for i, j in pairs])


def per_device(nj, nx, nh, queries, keys, values, out_grad):
    rows, width = queries.shape
    nz = 2 * nj
    scaling = 1.0 / math.sqrt(width)
    rate = scaling * math.log2(math.e)
    smem = pl.BlockSpec(memory_space=pltpu.SMEM)
    vmem = pl.BlockSpec(memory_space=pltpu.VMEM)
    own, mixed = pl.pallas_call(
        functools.partial(prepare_kernel, nh),
        out_shape=(
            jax.ShapeDtypeStruct((rows, 2 * width), BF16),
            jax.ShapeDtypeStruct((nj * nh, keys.shape[0], 2 * width), BF16),
        ),
        in_specs=[pl.BlockSpec(memory_space=pltpu.HBM)] * 4,
        out_specs=(vmem,) * 2,
        scratch_shapes=[pltpu.VMEM((2, *keys.shape), BF16), pltpu.SemaphoreType.DMA((4,))],
        compiler_params=pltpu.CompilerParams(vmem_limit_bytes=60 << 20),
        name="prepare",
    )(queries, out_grad, keys, values)
    other_own = swapped(own, nz)
    blocks = [own, shifted(own, "x", nx, 1)]
    blocks += [shifted(own, "x", nx, r) for r in range(2, nx)]
    blocks += [other_own] + [shifted(other_own, "x", nx, r) for r in range(1, nx)]
    kv = lax.all_to_all(mixed, ("zj", "head"), 0, 0, tiled=True)
    kv = kv.reshape(nj, rows, 2 * width)
    zj, zp, x = (lax.axis_index(a) for a in SEQ)
    other = jnp.where(zp == 0, jnp.where(zj == 0, nj, zj), lax.rem(zj + 1, nj))
    where = jnp.stack([zj, other, x, 1 - zp]).astype(jnp.int32)
    pairs = 7 * rows * nx * rows * width
    sent = (2 * nx, width + sum(PIECES) * 2 * nx, rows)
    units = (2 * nj - 1, rows, nx * rows)
    stat = pltpu.VMEM((2 * nx, len(PIECES), 2 * nx, rows), F32)
    gathered = [pltpu.VMEM((2, nx * rows, width), BF16)] * 2
    parts, scores = pl.pallas_call(
        functools.partial(forward_kernel, rate, nx),
        out_shape=(jax.ShapeDtypeStruct(sent, BF16), jax.ShapeDtypeStruct(units, F32)),
        in_specs=[smem] + [vmem] * (2 * nx + 1),
        out_specs=(vmem, vmem),
        scratch_shapes=[
            pltpu.VMEM((len(PIECES), 2 * nx, rows), F32),
            pltpu.VMEM((2, width, nx * rows), F32),
            pltpu.VMEM((2, 8, nx * rows), F32),
            pltpu.VMEM((2, 8, nx * rows), F32),
            *gathered,
        ],
        compiler_params=pltpu.CompilerParams(vmem_limit_bytes=VMEM),
        cost_estimate=pl.CostEstimate(flops=4 * pairs, bytes_accessed=2 << 20, transcendentals=0),
        name="forward",
    )(where, *blocks, kv)
    groups = [[z * nx + i for z in (m, (m + 1) % nz) for i in range(nx)] for m in range(1, nz, 2)]
    got = lax.all_to_all(parts, SEQ, 0, 0, axis_index_groups=groups, tiled=True)
    both = pl.pallas_call(
        functools.partial(backward_kernel, rate, scaling, nx),
        out_shape=(jax.ShapeDtypeStruct((width, 2 * rows), BF16),) * nx
        + (jax.ShapeDtypeStruct((rows, 2 * width), BF16),) * nj,
        in_specs=[smem] + [vmem] * (2 * nx + 3),
        out_specs=(vmem,) * (nx + nj),
        scratch_shapes=[
            pltpu.VMEM((2, width, nx * rows), F32),
            pltpu.VMEM((2, 1, nx * rows), F32),
            pltpu.VMEM((2, 1, nx * rows), F32),
            pltpu.VMEM(kv.shape, F32),
            stat,
            *gathered,
        ],
        compiler_params=pltpu.CompilerParams(vmem_limit_bytes=VMEM),
        cost_estimate=pl.CostEstimate(flops=10 * pairs, bytes_accessed=2 << 20, transcendentals=0),
        name="backward",
    )(where, *blocks, kv, got, scores)
    parts, dkv = both[:nx], both[nx:]
    parts = [parts[0]] + [shifted(parts[-r % nx], "x", nx, r) for r in range(1, nx)]
    dkv = [dkv[0]] + [shifted(dkv[r], "zj", nj, r) for r in range(1, nj)]
    attended = pl.pallas_call(
        functools.partial(mix_kernel, nx),
        out_shape=jax.ShapeDtypeStruct((rows, width), BF16),
        in_specs=[smem, vmem],
        out_specs=vmem,
        scratch_shapes=[stat],
        compiler_params=pltpu.CompilerParams(vmem_limit_bytes=8 << 20),
        name="mix",
    )(where, got)
    back = functools.reduce(jnp.add, [p[:, rows:].astype(F32) for p in parts])
    back = swapped(back.astype(BF16), nz)
    sums = pl.pallas_call(
        functools.partial(final_kernel, nx, nj),
        out_shape=(jax.ShapeDtypeStruct((rows, width), F32),) * 3,
        in_specs=[vmem] * (nx + nj + 1),
        out_specs=(vmem,) * 3,
        compiler_params=pltpu.CompilerParams(vmem_limit_bytes=8 << 20),
        name="final",
    )(*parts, back, *dkv)
    return attended, *sums


def solution(mesh):
    nh = mesh.shape["head"]
    split = Mesh(mesh.devices.reshape(4, 2, -1, nh), (*SEQ, "head"))
    return jax.shard_map(
        functools.partial(per_device, 4, split.shape["x"], nh),
        mesh=split,
        in_specs=(P(SEQ, "head"), P((*SEQ, "head"), None), P((*SEQ, "head"), None), P(SEQ, "head")),
        out_specs=(P(SEQ, "head"),) * 4,
        check_vma=False,
    )
```

profile of v0, /device:TPU:8, one launch (start us, length us, event | category | flops | bytes accessed | tf_op | source)
XLA Modules:
  0.0 89.2 jit_solution(4581616439221462341)
XLA Ops:
  0.6 1.8 %prepare.1 = (bf16[256,256]{1,0:T(8,128)(2,1)}, bf16[32,32,256]{2,1,0:T(8,128)(2,1)}) custom-call(bf16[256,128]{1,0:T(8,128)(2,1)} %q_ref.1, bf16[256,128]{1,0:T(8,128)(2,1)} %g_ref.1, bf16[32,1024]{1,0:T(8,128)(2,1)} %k_ref.1, bf16[32,1024]{1,0:T(8,128)(2,1)} %v_ref.1), custom_call_target="tpu_custom_call" | custom-call | tf_op jit(solution)/shard_map/prepare/pallas_call | solution.py:236
  2.4 11.7 %all-to-all-start = ((bf16[32,32,256]{2,1,0:T(8,128)(2,1)}), bf16[32,32,256]{2,1,0:T(8,128)(2,1)S(1)}, u32[]{:S(2)}, u32[]{:S(2)}) async-start(bf16[32,32,256]{2,1,0:T(8,128)(2,1)} %get-tuple-element.20), calls=%async_computation | async-start | bytes 1048576 | tf_op jit(solution)/shard_map/all_to_all | solution.py:252
  14.2 3.3 %collective-permute-start.3 = (bf16[256,256]{1,0:T(8,128)(2,1)}, bf16[256,256]{1,0:T(8,128)(2,1)S(1)}, u32[]{:S(2)}, u32[]{:S(2)}) collective-permute-start(bf16[256,256]{1,0:T(8,128)(2,1)} %get-tuple-element.19.refs_0_), channel_id=1, source_target_pairs={{32,64},{96,128},{160,192},{224,0},{64,32},{128,96},{192,160},{0,2... | collective-permute-start | bytes 393224 | tf_op jit(solution)/shard_map/ppermute | solution.py:226
  17.4 2.8 %collective-permute-start.2 = (bf16[256,256]{1,0:T(8,128)(2,1)}, bf16[256,256]{1,0:T(8,128)(2,1)S(1)}, u32[]{:S(2)}, u32[]{:S(2)}) collective-permute-start(bf16[256,256]{1,0:T(8,128)(2,1)} %get-tuple-element.19.refs_0_), channel_id=1, source_target_pairs={{0,24},{8,0},{16,8},{24,16},{1,25},{9,1},{17,9},{25,17},{2,26},{10... | collective-permute-start | bytes 393224 | tf_op jit(solution)/shard_map/ppermute | solution.py:221
  20.2 0.8 collective-permute-start.1
  21.0 0.9 collective-permute-start
  21.9 10.6 %collective-permute-done.3.refs_4_ = bf16[256,256]{1,0:T(8,128)(2,1)S(1)} collective-permute-done((bf16[256,256]{1,0:T(8,128)(2,1)}, bf16[256,256]{1,0:T(8,128)(2,1)S(1)}, u32[]{:S(2)}, u32[]{:S(2)}) %collective-permute-start.3) | collective-permute-done | bytes 131104 | tf_op jit(solution)/shard_map/ppermute | solution.py:226
  32.5 2.8 %collective-permute-start.6 = (bf16[256,256]{1,0:T(8,128)(2,1)S(1)}, bf16[256,256]{1,0:T(8,128)(2,1)S(1)}, u32[]{:S(2)}, u32[]{:S(2)}) collective-permute-start(bf16[256,256]{1,0:T(8,128)(2,1)S(1)} %collective-permute-done.3.refs_4_), channel_id=1, source_target_pairs={{0,24},{8,0},{16,8},{24,16},{1,25},{9,1},{17,9},{25,17},{2,26},{10... | collective-permute-start | bytes 393224 | tf_op jit(solution)/shard_map/ppermute | solution.py:221
  35.2 0.8 collective-permute-start.5
  36.0 0.0 collective-permute-done.2.refs_3_
  36.0 0.9 collective-permute-start.4
  36.9 0.1 pad_add_fusion.where_ref
  37.0 0.0 collective-permute-done.1.refs_2_
  37.0 0.0 collective-permute-done.refs_1_
  37.0 3.6 %collective-permute-done.6.refs_7_ = bf16[256,256]{1,0:T(8,128)(2,1)S(1)} collective-permute-done((bf16[256,256]{1,0:T(8,128)(2,1)S(1)}, bf16[256,256]{1,0:T(8,128)(2,1)S(1)}, u32[]{:S(2)}, u32[]{:S(2)}) %collective-permute-start.6) | collective-permute-done | bytes 131104 | tf_op jit(solution)/shard_map/ppermute | solution.py:221
  40.6 2.3 %collective-permute-done.5.refs_6_ = bf16[256,256]{1,0:T(8,128)(2,1)S(1)} collective-permute-done((bf16[256,256]{1,0:T(8,128)(2,1)S(1)}, bf16[256,256]{1,0:T(8,128)(2,1)S(1)}, u32[]{:S(2)}, u32[]{:S(2)}) %collective-permute-start.5) | collective-permute-done | bytes 131104 | tf_op jit(solution)/shard_map/ppermute | solution.py:221
  42.8 1.4 %collective-permute-done.4.refs_5_ = bf16[256,256]{1,0:T(8,128)(2,1)S(1)} collective-permute-done((bf16[256,256]{1,0:T(8,128)(2,1)S(1)}, bf16[256,256]{1,0:T(8,128)(2,1)S(1)}, u32[]{:S(2)}, u32[]{:S(2)}) %collective-permute-start.4) | collective-permute-done | bytes 131104 | tf_op jit(solution)/shard_map/ppermute | solution.py:221
  44.2 0.0 all-to-all-done
  44.2 0.0 copy-start
  44.2 0.9 %copy-done = bf16[256,256]{1,0:T(8,128)(2,1)S(1)} copy-done((bf16[256,256]{1,0:T(8,128)(2,1)S(1)}, bf16[256,256]{1,0:T(8,128)(2,1)}, u32[]{:S(2)}) %copy-start) | copy-done | bytes 131096
  45.1 4.3 %forward.1 = (bf16[8,184,256]{2,1,0:T(8,128)(2,1)S(1)}, f32[7,256,1024]{2,1,0:T(8,128)S(1)}) custom-call(s32[4]{0:T(128)S(1)} %pad_add_fusion.where_ref, bf16[256,256]{1,0:T(8,128)(2,1)S(1)} %copy-done, bf16[256,256]{1,0:T(8,128)(2,1)S(1)} %collective-permute-done.refs_1_, bf16[256,256]{1,0:T(8,128)(2,1)S(1)} %collective-permute-done.1.refs_2_, ...), custom_call_target="tpu_custom_call" | custom-call | flops 939524096 | bytes 2097152 | tf_op jit(solution)/shard_map/forward/pallas_call | solution.py:262
  49.4 15.1 %all_to_all.10.got_ref.refs_9_ = bf16[8,184,256]{2,1,0:T(8,128)(2,1)S(1)} all-to-all(bf16[8,184,256]{2,1,0:T(8,128)(2,1)S(1)} %get-tuple-element.21), channel_id=1, replica_groups={{32,40,48,56,64,72,80,88},{96,104,112,120,128,136,144,152},{160,168,176..., dimensions={0} | all-to-all | bytes 1507328 | tf_op jit(solution)/shard_map/all_to_all | solution.py:279
  64.6 4.6 %backward.1 = (bf16[128,512]{1,0:T(8,128)(2,1)S(1)}, bf16[128,512]{1,0:T(8,128)(2,1)S(1)}, bf16[128,512]{1,0:T(8,128)(2,1)S(1)}, bf16[128,512]{1,0:T(8,128)(2,1)...) custom-call(s32[4]{0:T(128)S(1)} %pad_add_fusion.where_ref, ...), custom_call_target="tpu_custom_call" | custom-call | flops 2348810240 | bytes 2097152 | tf_op jit(solution)/shard_map/backward/pallas_call | solution.py:280
  69.2 0.9 %collective-permute-start.7 = (bf16[128,512]{1,0:T(8,128)(2,1)S(1)}, bf16[128,512]{1,0:T(8,128)(2,1)S(1)}, u32[]{:S(2)}, u32[]{:S(2)}) collective-permute-start(bf16[128,512]{1,0:T(8,128)(2,1)S(1)} %get-tuple-element.24), channel_id=1, source_target_pairs={{0,8},{8,16},{16,24},{24,0},{1,9},{9,17},{17,25},{25,1},{2,10},{10... | collective-permute-start | bytes 393224 | tf_op jit(solution)/shard_map/ppermute | solution.py:221
  70.1 2.1 %collective-permute-start.8 = (bf16[128,512]{1,0:T(8,128)(2,1)S(1)}, bf16[128,512]{1,0:T(8,128)(2,1)S(1)}, u32[]{:S(2)}, u32[]{:S(2)}) collective-permute-start(bf16[128,512]{1,0:T(8,128)(2,1)S(1)} %get-tuple-element.25), channel_id=1, source_target_pairs={{0,16},{8,24},{16,0},{24,8},{1,17},{9,25},{17,1},{25,9},{2,18},{10... | collective-permute-start | bytes 393224 | tf_op jit(solution)/shard_map/ppermute | solution.py:221
  72.2 0.9 collective-permute-start.9
  73.0 0.0 collective-permute-start.11
  73.0 6.1 %collective-permute-start.12 = (bf16[256,256]{1,0:T(8,128)(2,1)S(1)}, bf16[256,256]{1,0:T(8,128)(2,1)S(1)}, u32[]{:S(2)}, u32[]{:S(2)}) collective-permute-start(bf16[256,256]{1,0:T(8,128)(2,1)S(1)} %get-tuple-element.29), channel_id=1, source_target_pairs={{0,128},{64,192},{128,0},{192,64},{1,129},{65,193},{129,1},{193,65... | collective-permute-start | bytes 393224 | tf_op jit(solution)/shard_map/ppermute | solution.py:221
  79.1 0.0 collective-permute-done.7.refs_1_
  79.1 1.8 %collective-permute-start.13 = (bf16[256,256]{1,0:T(8,128)(2,1)S(1)}, bf16[256,256]{1,0:T(8,128)(2,1)S(1)}, u32[]{:S(2)}, u32[]{:S(2)}) collective-permute-start(bf16[256,256]{1,0:T(8,128)(2,1)S(1)} %get-tuple-element.30), channel_id=1, source_target_pairs={{0,192},{64,0},{128,64},{192,128},{1,193},{65,1},{129,65},{193,129... | collective-permute-start | bytes 393224 | tf_op jit(solution)/shard_map/ppermute | solution.py:221
  80.9 0.0 collective-permute-done.8.refs_2_
  80.9 0.0 collective-permute-done.9.refs_3_
  81.0 0.5 collective-permute-start.10
  81.5 1.4 %mix.1 = bf16[256,128]{1,0:T(8,128)(2,1)} custom-call(s32[4]{0:T(128)S(1)} %pad_add_fusion.where_ref, bf16[8,184,256]{2,1,0:T(8,128)(2,1)S(1)} %all_to_all.10.got_ref.refs_9_), custom_call_target="tpu_custom_call" | custom-call | tf_op jit(solution)/shard_map/mix/pallas_call | solution.py:301
  82.9 0.6 collective-permute-done.11.refs_6_
  83.4 4.1 %collective-permute-done.12.refs_7_ = bf16[256,256]{1,0:T(8,128)(2,1)S(1)} collective-permute-done((bf16[256,256]{1,0:T(8,128)(2,1)S(1)}, bf16[256,256]{1,0:T(8,128)(2,1)S(1)}, u32[]{:S(2)}, u32[]{:S(2)}) %collective-permute-start.12) | collective-permute-done | bytes 131104 | tf_op jit(solution)/shard_map/ppermute | solution.py:221
  87.5 0.9 %collective-permute-done.13.refs_8_ = bf16[256,256]{1,0:T(8,128)(2,1)S(1)} collective-permute-done((bf16[256,256]{1,0:T(8,128)(2,1)S(1)}, bf16[256,256]{1,0:T(8,128)(2,1)S(1)}, u32[]{:S(2)}, u32[]{:S(2)}) %collective-permute-start.13) | collective-permute-done | bytes 131104 | tf_op jit(solution)/shard_map/ppermute | solution.py:221
  88.4 0.0 collective-permute-done.10.refs_4_
  88.4 0.8 final.1
  (1 shorter events, 0.0 us)
Async XLA Ops:
  2.4 41.8 %all-to-all-start = ((bf16[32,32,256]{2,1,0:T(8,128)(2,1)}), bf16[32,32,256]{2,1,0:T(8,128)(2,1)S(1)}, u32[]{:S(2)}, u32[]{:S(2)}) async-start(bf16[32,32,256]{2,1,0:T(8,128)(2,1)} %get-tuple-element.20), calls=%async_computation | async-start | bytes 1048576 | tf_op jit(solution)/shard_map/all_to_all | solution.py:252
  14.2 18.3 %collective-permute-start.3 = (bf16[256,256]{1,0:T(8,128)(2,1)}, bf16[256,256]{1,0:T(8,128)(2,1)S(1)}, u32[]{:S(2)}, u32[]{:S(2)}) collective-permute-start(bf16[256,256]{1,0:T(8,128)(2,1)} %get-tuple-element.19.refs_0_), channel_id=1, source_target_pairs={{32,64},{96,128},{160,192},{224,0},{64,32},{128,96},{192,160},{0,2... | collective-permute-start | bytes 393224 | tf_op jit(solution)/shard_map/ppermute | solution.py:226
  17.4 18.6 %collective-permute-start.2 = (bf16[256,256]{1,0:T(8,128)(2,1)}, bf16[256,256]{1,0:T(8,128)(2,1)S(1)}, u32[]{:S(2)}, u32[]{:S(2)}) collective-permute-start(bf16[256,256]{1,0:T(8,128)(2,1)} %get-tuple-element.19.refs_0_), channel_id=1, source_target_pairs={{0,24},{8,0},{16,8},{24,16},{1,25},{9,1},{17,9},{25,17},{2,26},{10... | collective-permute-start | bytes 393224 | tf_op jit(solution)/shard_map/ppermute | solution.py:221
  20.2 16.8 %collective-permute-start.1 = (bf16[256,256]{1,0:T(8,128)(2,1)}, bf16[256,256]{1,0:T(8,128)(2,1)S(1)}, u32[]{:S(2)}, u32[]{:S(2)}) collective-permute-start(bf16[256,256]{1,0:T(8,128)(2,1)} %get-tuple-element.19.refs_0_), channel_id=1, source_target_pairs={{0,16},{8,24},{16,0},{24,8},{1,17},{9,25},{17,1},{25,9},{2,18},{10... | collective-permute-start | bytes 393224 | tf_op jit(solution)/shard_map/ppermute | solution.py:221
  21.0 16.0 %collective-permute-start = (bf16[256,256]{1,0:T(8,128)(2,1)}, bf16[256,256]{1,0:T(8,128)(2,1)S(1)}, u32[]{:S(2)}, u32[]{:S(2)}) collective-permute-start(bf16[256,256]{1,0:T(8,128)(2,1)} %get-tuple-element.19.refs_0_), channel_id=1, source_target_pairs={{0,8},{8,16},{16,24},{24,0},{1,9},{9,17},{17,25},{25,1},{2,10},{10... | collective-permute-start | bytes 393224 | tf_op jit(solution)/shard_map/ppermute | solution.py:221
  32.5 8.1 %collective-permute-start.6 = (bf16[256,256]{1,0:T(8,128)(2,1)S(1)}, bf16[256,256]{1,0:T(8,128)(2,1)S(1)}, u32[]{:S(2)}, u32[]{:S(2)}) collective-permute-start(bf16[256,256]{1,0:T(8,128)(2,1)S(1)} %collective-permute-done.3.refs_4_), channel_id=1, source_target_pairs={{0,24},{8,0},{16,8},{24,16},{1,25},{9,1},{17,9},{25,17},{2,26},{10... | collective-permute-start | bytes 393224 | tf_op jit(solution)/shard_map/ppermute | solution.py:221
  35.2 7.6 %collective-permute-start.5 = (bf16[256,256]{1,0:T(8,128)(2,1)S(1)}, bf16[256,256]{1,0:T(8,128)(2,1)S(1)}, u32[]{:S(2)}, u32[]{:S(2)}) collective-permute-start(bf16[256,256]{1,0:T(8,128)(2,1)S(1)} %collective-permute-done.3.refs_4_), channel_id=1, source_target_pairs={{0,16},{8,24},{16,0},{24,8},{1,17},{9,25},{17,1},{25,9},{2,18},{10... | collective-permute-start | bytes 393224 | tf_op jit(solution)/shard_map/ppermute | solution.py:221
  36.0 8.2 %collective-permute-start.4 = (bf16[256,256]{1,0:T(8,128)(2,1)S(1)}, bf16[256,256]{1,0:T(8,128)(2,1)S(1)}, u32[]{:S(2)}, u32[]{:S(2)}) collective-permute-start(bf16[256,256]{1,0:T(8,128)(2,1)S(1)} %collective-permute-done.3.refs_4_), channel_id=1, source_target_pairs={{0,8},{8,16},{16,24},{24,0},{1,9},{9,17},{17,25},{25,1},{2,10},{10... | collective-permute-start | bytes 393224 | tf_op jit(solution)/shard_map/ppermute | solution.py:221
  44.2 0.9 %copy-start = (bf16[256,256]{1,0:T(8,128)(2,1)S(1)}, bf16[256,256]{1,0:T(8,128)(2,1)}, u32[]{:S(2)}) copy-start(bf16[256,256]{1,0:T(8,128)(2,1)} %get-tuple-element.19.refs_0_) | copy-start | bytes 393220
  69.2 10.0 %collective-permute-start.7 = (bf16[128,512]{1,0:T(8,128)(2,1)S(1)}, bf16[128,512]{1,0:T(8,128)(2,1)S(1)}, u32[]{:S(2)}, u32[]{:S(2)}) collective-permute-start(bf16[128,512]{1,0:T(8,128)(2,1)S(1)} %get-tuple-element.24), channel_id=1, source_target_pairs={{0,8},{8,16},{16,24},{24,0},{1,9},{9,17},{17,25},{25,1},{2,10},{10... | collective-permute-start | bytes 393224 | tf_op jit(solution)/shard_map/ppermute | solution.py:221
  70.1 10.8 %collective-permute-start.8 = (bf16[128,512]{1,0:T(8,128)(2,1)S(1)}, bf16[128,512]{1,0:T(8,128)(2,1)S(1)}, u32[]{:S(2)}, u32[]{:S(2)}) collective-permute-start(bf16[128,512]{1,0:T(8,128)(2,1)S(1)} %get-tuple-element.25), channel_id=1, source_target_pairs={{0,16},{8,24},{16,0},{24,8},{1,17},{9,25},{17,1},{25,9},{2,18},{10... | collective-permute-start | bytes 393224 | tf_op jit(solution)/shard_map/ppermute | solution.py:221
  72.2 8.8 %collective-permute-start.9 = (bf16[128,512]{1,0:T(8,128)(2,1)S(1)}, bf16[128,512]{1,0:T(8,128)(2,1)S(1)}, u32[]{:S(2)}, u32[]{:S(2)}) collective-permute-start(bf16[128,512]{1,0:T(8,128)(2,1)S(1)} %get-tuple-element.26), channel_id=1, source_target_pairs={{0,24},{8,0},{16,8},{24,16},{1,25},{9,1},{17,9},{25,17},{2,26},{10... | collective-permute-start | bytes 393224 | tf_op jit(solution)/shard_map/ppermute | solution.py:221
  73.0 10.4 %collective-permute-start.11 = (bf16[256,256]{1,0:T(8,128)(2,1)S(1)}, bf16[256,256]{1,0:T(8,128)(2,1)S(1)}, u32[]{:S(2)}, u32[]{:S(2)}) collective-permute-start(bf16[256,256]{1,0:T(8,128)(2,1)S(1)} %get-tuple-element.28), channel_id=1, source_target_pairs={{0,64},{64,128},{128,192},{192,0},{1,65},{65,129},{129,193},{193,1... | collective-permute-start | bytes 393224 | tf_op jit(solution)/shard_map/ppermute | solution.py:221
  73.0 14.5 %collective-permute-start.12 = (bf16[256,256]{1,0:T(8,128)(2,1)S(1)}, bf16[256,256]{1,0:T(8,128)(2,1)S(1)}, u32[]{:S(2)}, u32[]{:S(2)}) collective-permute-start(bf16[256,256]{1,0:T(8,128)(2,1)S(1)} %get-tuple-element.29), channel_id=1, source_target_pairs={{0,128},{64,192},{128,0},{192,64},{1,129},{65,193},{129,1},{193,65... | collective-permute-start | bytes 393224 | tf_op jit(solution)/shard_map/ppermute | solution.py:221
  79.1 9.3 %collective-permute-start.13 = (bf16[256,256]{1,0:T(8,128)(2,1)S(1)}, bf16[256,256]{1,0:T(8,128)(2,1)S(1)}, u32[]{:S(2)}, u32[]{:S(2)}) collective-permute-start(bf16[256,256]{1,0:T(8,128)(2,1)S(1)} %get-tuple-element.30), channel_id=1, source_target_pairs={{0,192},{64,0},{128,64},{192,128},{1,193},{65,1},{129,65},{193,129... | collective-permute-start | bytes 393224 | tf_op jit(solution)/shard_map/ppermute | solution.py:221
  81.0 7.4 %collective-permute-start.10 = (bf16[128,256]{1,0:T(8,128)(2,1)S(1)}, bf16[128,256]{1,0:T(8,128)(2,1)S(1)}, u32[]{:S(2)}, u32[]{:S(2)}) collective-permute-start(bf16[128,256]{1,0:T(8,128)(2,1)S(1)} %add_convert_fusion), channel_id=1, source_target_pairs={{32,64},{96,128},{160,192},{224,0},{64,32},{128,96},{192,160},{0,2... | collective-permute-start | bytes 196616 | tf_op jit(solution)/shard_map/ppermute | solution.py:226
where the time goes:
time: 90.1 us; the launch traced here: 89.2 us
  starting transfers between devices  36.1 us (40%)
  waiting for transfers between devices  23.4 us (26%)
  blocking collectives  15.1 us (17%)
  Pallas kernels  12.9 us (14%)
  local copies, waits for them, and re-layouts  0.91 us (1%)
    ppermute x12, starting transfers between devices, shifted(): lax.ppermute(value, axis, [(i, (i + step) % count) for i in range(count)])  20.7 us
    all_to_all x1, blocking collectives, per_device(): got = lax.all_to_all(parts, SEQ, 0, 0, axis_index_groups=groups, tiled=True)  15.1 us
    ppermute x12, waiting for transfers between devices, shifted(): lax.ppermute(value, axis, [(i, (i + step) % count) for i in range(count)])  12.8 us
    all_to_all x1, starting transfers between devices, per_device(): kv = lax.all_to_all(mixed, ('zj', 'head'), 0, 0, tiled=True)  11.7 us
    ppermute x2, waiting for transfers between devices, swapped(): return lax.ppermute(value, Z, pairs + [(j, i) for i, j in pairs])  10.6 us
    pallas_call x1, Pallas kernels, per_device(): pl.pallas_call(functools.partial(backward_kernel, rate, scaling, nx), out...  4.57 us
    pallas_call x1, Pallas kernels, per_device(): pl.pallas_call(functools.partial(forward_kernel, rate, nx), out_shape=(ja...  4.3 us
    ppermute x2, starting transfers between devices, swapped(): return lax.ppermute(value, Z, pairs + [(j, i) for i, j in pairs])  3.76 us
  transfers between devices with their start and end apart: 15, of which 7 were waited for; matrix products, arithmetic and copies ran while one was open for 0% of the time, Pallas kernels for 2%

commit v1 on v0

v1 whole, which is shorter than its diff:
```python
import functools
import math

import jax
import jax.numpy as jnp
from jax import lax
from jax.experimental import pallas as pl
from jax.experimental.pallas import tpu as pltpu
from jax.sharding import Mesh
from jax.sharding import PartitionSpec as P

Z = ("zj", "zp")
SEQ = (*Z, "x")
VMEM = 24 << 20
LOW = -1e30
F32 = jnp.float32
BF16 = jnp.bfloat16
NT = (((1,), (1,)), ((), ()))
TN = (((0,), (0,)), ((), ()))
NN = (((1,), (0,)), ((), ()))


def dot(a, b, dims):
    return lax.dot_general(a, b, dims, preferred_element_type=F32)


def allowed_pairs(rows, key_block, query_block):
    key_pos = lax.broadcasted_iota(jnp.int32, (rows, rows), 0) + key_block * rows
    query_pos = lax.broadcasted_iota(jnp.int32, (rows, rows), 1) + query_block * rows
    return key_pos <= query_pos


def diagonal(rows, x, nx):
    oks = [allowed_pairs(rows, x, lax.rem(x - r + nx, nx)) for r in range(nx)]
    return jnp.concatenate(oks, axis=1)


def prepare_kernel(nh, q_ref, g_ref, k_ref, v_ref, own_ref, mixed_ref, kv_ref, sems):
    width = q_ref.shape[1]
    moves = [
        pltpu.make_async_copy(k_ref, kv_ref.at[0], sems.at[0]),
        pltpu.make_async_copy(v_ref, kv_ref.at[1], sems.at[1]),
        pltpu.make_async_copy(q_ref, own_ref.at[:, :width], sems.at[2]),
        pltpu.make_async_copy(g_ref, own_ref.at[:, width:], sems.at[3]),
    ]
    for move in moves:
        move.start()
    for part in range(2):
        moves[part].wait()
        for at in range(mixed_ref.shape[0]):
            cols = slice(at % nh * width, (at % nh + 1) * width)
            mixed_ref[at, :, part * width : (part + 1) * width] = kv_ref[part, :, cols]
    moves[2].wait()
    moves[3].wait()


def gather_blocks(q_refs, query_ref, grad_ref):
    rows, width = q_refs[0].shape[0], q_refs[0].shape[1] // 2
    count = (len(q_refs) + 1) // 2
    for at, ref in enumerate(q_refs, 1):
        side, r = divmod(at, count)
        query_ref[side, r * rows : (r + 1) * rows, :] = ref[:, :width]
        grad_ref[side, r * rows : (r + 1) * rows, :] = ref[:, width:]


def each_unit(where_ref, last, unit):
    own, full = where_ref[0], where_ref[0] + where_ref[1]

    def whole(f, lane):
        side = jnp.where(f >= own, 1, 0)
        unit(f, side, f - side * own, False, lane)

    @pl.loop(0, full // 2)
    def _(i):
        whole(2 * i, 0)
        whole(2 * i + 1, 1)

    @pl.when(full % 2 == 1)
    def _():
        whole(full - 1, 0)
        unit(last, 0, own, True, 1)

    @pl.when(full % 2 == 0)
    def _():
        unit(last, 0, own, True, 0)


def folded(value, op):
    return op(value.reshape(value.shape[0] // 8, 8, value.shape[1]), axis=0)


def forward_kernel(rate, nx, where_ref, *refs):
    n = 2 * nx
    (own_q_ref, own_g_ref), q_refs, kv_ref, refs = refs[:2], refs[2 : n + 1], refs[n + 1], refs[n + 2 :]
    out_refs, (send_ref, query_ref, grad_ref), refs = refs[:nx], refs[nx : nx + 3], refs[nx + 3 :]
    s_ref, stat_ref, o_ref, m_ref, l_ref, sems = refs
    x, even = where_ref[2], where_ref[3]
    rows, width = kv_ref.shape[1], kv_ref.shape[2] // 2
    moves = [
        pltpu.make_async_copy(own_q_ref, query_ref.at[0, :rows, :], sems.at[0]),
        pltpu.make_async_copy(own_g_ref, grad_ref.at[0, :rows, :], sems.at[1]),
    ]
    for move in moves:
        move.start()
    gather_blocks(q_refs, query_ref, grad_ref)
    m_ref[...] = jnp.full_like(m_ref, LOW)
    l_ref[...] = jnp.zeros_like(l_ref)
    o_ref[...] = jnp.zeros_like(o_ref)
    for move in moves:
        move.wait()

    def score(u, side, j, masked, lane):
        s = dot(kv_ref[j, :, :width], query_ref[side], NT)
        if masked:
            s = jnp.where(diagonal(rows, x, nx), s, LOW)
        s_ref[u] = s
        m_ref[lane, side] = jnp.maximum(m_ref[lane, side], folded(s, jnp.max))

    def weigh(u, side, j, masked, lane):
        p = jnp.exp2((s_ref[u] - m_ref[0, side, 0:1, :]) * rate)
        l_ref[lane, side] += folded(p, jnp.sum)
        o_ref[lane, side] += dot(kv_ref[j, :, width:], p.astype(BF16), TN)

    last = s_ref.shape[0] - 1
    each_unit(where_ref, last, score)
    for side in range(2):
        both = jnp.maximum(m_ref[0, side], m_ref[1, side])
        m_ref[0, side, 0:1, :] = jnp.maximum(jnp.max(both, axis=0, keepdims=True), LOW / 2)
    each_unit(where_ref, last, weigh)
    for side in range(2):
        total = jnp.sum(l_ref[0, side] + l_ref[1, side], axis=0, keepdims=True)
        o_ref[0, side] += o_ref[1, side]
        grads = jnp.transpose(grad_ref[side].astype(F32))
        inner = jnp.sum(grads * o_ref[0, side], axis=0, keepdims=True)
        for r in range(nx):
            cols = slice(r * rows, (r + 1) * rows)
            at = (side ^ even) * nx + lax.rem(x - r + nx, nx)
            stat_ref[pl.ds(at, 1), :] = m_ref[0, side, 0:1, cols] * rate
            stat_ref[pl.ds(n + at, 1), :] = total[:, cols]
            stat_ref[pl.ds(2 * n + at, 1), :] = inner[:, cols]
            out_refs[r][:, side * rows : (side + 1) * rows] = o_ref[0, side, :, cols].astype(BF16)
    for to in range(n):
        send_ref[to] = stat_ref[...]


def backward_kernel(rate, scaling, nx, where_ref, *refs):
    n = 2 * nx
    (query_ref, grad_ref, kv_ref, got_ref), refs = refs[:4], refs[4:]
    nj = kv_ref.shape[0]
    out_refs, key_refs, refs = refs[:nx], refs[nx : nx + nj], refs[nx + nj :]
    dq_ref, norm_ref, delta_ref, acc_ref, row_ref = refs
    x, even = where_ref[2], where_ref[3]
    rows, width = kv_ref.shape[1], kv_ref.shape[2] // 2
    dq_ref[...] = jnp.zeros_like(dq_ref)
    acc_ref[...] = jnp.zeros_like(acc_ref)
    maxima = [got_ref[i, :n] for i in range(n)]
    top = functools.reduce(jnp.maximum, maxima)
    shares = [jnp.exp2(m - top) for m in maxima]
    total = sum(got_ref[i, n : 2 * n] * w for i, w in enumerate(shares))
    delta = sum(got_ref[i, 2 * n :] * w for i, w in enumerate(shares))
    row_ref[0] = top + jnp.log2(total)
    row_ref[1] = delta / total
    for at in range(n):
        side, r = divmod(at, nx)
        cols = slice(r * rows, (r + 1) * rows)
        row = pl.ds((side ^ even) * nx + lax.rem(x - r + nx, nx), 1)
        norm_ref[side, :, cols] = row_ref[0, row, :]
        delta_ref[side, :, cols] = row_ref[1, row, :]

    def unit(u, side, j, masked, lane):
        k, v = kv_ref[j, :, :width], kv_ref[j, :, width:]
        s = dot(k, query_ref[side], NT)
        if masked:
            s = jnp.where(diagonal(rows, x, nx), s, LOW)
        p = jnp.exp2(s * rate - norm_ref[side])
        ds = (p * (dot(v, grad_ref[side], NT) - delta_ref[side])).astype(BF16)
        acc_ref[lane, j, :, width:] += dot(p.astype(BF16), grad_ref[side], NN)
        acc_ref[lane, j, :, :width] += dot(ds, query_ref[side], NN)
        dq_ref[lane, side] += dot(k, ds, TN)

    each_unit(where_ref, 0, unit)
    for step in range(nj):
        to = lax.rem(where_ref[0] + step, nj)
        both = acc_ref[0, to] + acc_ref[1, to]
        key_refs[step][:, :width] = (both[:, :width] * scaling).astype(BF16)
        key_refs[step][:, width:] = both[:, width:].astype(BF16)
    for at in range(n):
        side, r = divmod(at, nx)
        cols = slice(r * rows, (r + 1) * rows)
        out_refs[r][:, side * rows : (side + 1) * rows] = (
            (dq_ref[0, side, :, cols] + dq_ref[1, side, :, cols]) * scaling
        ).astype(BF16)


def mix_kernel(nx, where_ref, got_ref, *refs):
    part_refs, outs = refs[:nx], refs[nx:]
    x, even = where_ref[2], where_ref[3]
    n = 2 * nx
    width, rows = part_refs[0].shape[0], part_refs[0].shape[1] // 2
    for side in range(2):
        at = (side ^ even) * nx + x
        maxima = [got_ref[i, pl.ds(at, 1), :] for i in range(n)]
        top = functools.reduce(jnp.maximum, maxima)
        sums = [got_ref[i, pl.ds(n + at, 1), :] * jnp.exp2(m - top) for i, m in enumerate(maxima)]
        total = sum(sums)
        mixed = jnp.zeros((width, rows), F32)
        for e in range(nx):
            peer = even * nx + lax.rem(x - e + nx, nx)
            share = jnp.exp2(got_ref[peer, pl.ds(at, 1), :] - top) / total
            mixed = mixed + share * part_refs[e][:, side * rows : (side + 1) * rows]
        outs[side][...] = mixed.astype(outs[side].dtype)


def final_kernel(nx, nj, *refs):
    part_refs, (near_ref, back_ref), key_refs, outs = refs[:nx], refs[nx : nx + 2], refs[nx + 2 : -4], refs[-4:]
    rows, width = outs[0].shape
    dq = back_ref[:, :rows].astype(F32)
    for part in part_refs:
        dq = dq + part[:, :rows]
    outs[0][...] = jnp.transpose(near_ref[...] + back_ref[:, rows:]).astype(BF16)
    outs[1][...] = jnp.transpose(dq)
    total = key_refs[0][...].astype(F32)
    for j in range(1, nj):
        total = total + key_refs[j][...]
    outs[2][...] = total[:, :width]
    outs[3][...] = total[:, width:]


def shifted(value, axis, count, step):
    return lax.ppermute(value, axis, [(i, (i + step) % count) for i in range(count)])


def swapped(value, count):
    pairs = [(i, (i + 1) % count) for i in range(1, count, 2)]
    return lax.ppermute(value, Z, pairs + [(j, i) for i, j in pairs])


def per_device(nj, nx, nh, queries, keys, values, out_grad):
    rows, width = queries.shape
    nz = 2 * nj
    scaling = 1.0 / math.sqrt(width)
    rate = scaling * math.log2(math.e)
    smem = pl.BlockSpec(memory_space=pltpu.SMEM)
    vmem = pl.BlockSpec(memory_space=pltpu.VMEM)
    own, mixed = pl.pallas_call(
        functools.partial(prepare_kernel, nh),
        out_shape=(
            jax.ShapeDtypeStruct((rows, 2 * width), BF16),
            jax.ShapeDtypeStruct((nj * nh, keys.shape[0], 2 * width), BF16),
        ),
        in_specs=[pl.BlockSpec(memory_space=pltpu.HBM)] * 4,
        out_specs=(vmem,) * 2,
        scratch_shapes=[pltpu.VMEM((2, *keys.shape), BF16), pltpu.SemaphoreType.DMA((4,))],
        compiler_params=pltpu.CompilerParams(vmem_limit_bytes=60 << 20),
        name="prepare",
    )(queries, out_grad, keys, values)
    other_own = swapped(own, nz)
    blocks = [own, shifted(own, "x", nx, 1)]
    blocks += [shifted(own, "x", nx, r) for r in range(2, nx)]
    blocks += [other_own] + [shifted(other_own, "x", nx, r) for r in range(1, nx)]
    kv = lax.all_to_all(mixed, ("zj", "head"), 0, 0, tiled=True)
    kv = kv.reshape(nj, rows, 2 * width)
    zj, zp, x = (lax.axis_index(a) for a in SEQ)
    other = jnp.where(zp == 0, jnp.where(zj == 0, nj, zj), lax.rem(zj + 1, nj))
    where = jnp.stack([zj, other, x, 1 - zp]).astype(jnp.int32)
    pairs = 7 * rows * nx * rows * width
    units = (2 * nj - 1, rows, nx * rows)
    stat = (6 * nx, rows)
    gathered = (2, nx * rows, width)
    hbm = pl.BlockSpec(memory_space=pltpu.HBM)
    *offers, sent, all_q, all_g = pl.pallas_call(
        functools.partial(forward_kernel, rate, nx),
        out_shape=(jax.ShapeDtypeStruct((width, 2 * rows), BF16),) * nx
        + (jax.ShapeDtypeStruct((2 * nx, *stat), F32),)
        + (jax.ShapeDtypeStruct(gathered, BF16),) * 2,
        in_specs=[smem, hbm, hbm] + [vmem] * (2 * nx),
        out_specs=(vmem,) * (nx + 3),
        scratch_shapes=[
            pltpu.VMEM(units, F32),
            pltpu.VMEM(stat, F32),
            pltpu.VMEM((2, 2, width, nx * rows), F32),
            pltpu.VMEM((2, 2, 8, nx * rows), F32),
            pltpu.VMEM((2, 2, 8, nx * rows), F32),
            pltpu.SemaphoreType.DMA((2,)),
        ],
        compiler_params=pltpu.CompilerParams(vmem_limit_bytes=VMEM),
        cost_estimate=pl.CostEstimate(flops=4 * pairs, bytes_accessed=2 << 20, transcendentals=0),
        name="forward",
    )(where, queries, out_grad, *blocks[1:], kv)
    groups = [[z * nx + i for z in (m, (m + 1) % nz) for i in range(nx)] for m in range(1, nz, 2)]
    got = lax.all_to_all(sent, SEQ, 0, 0, axis_index_groups=groups, tiled=True)
    offers = [offers[0]] + [shifted(offers[-r % nx], "x", nx, r) for r in range(1, nx)]
    both = pl.pallas_call(
        functools.partial(backward_kernel, rate, scaling, nx),
        out_shape=(jax.ShapeDtypeStruct((width, 2 * rows), BF16),) * nx
        + (jax.ShapeDtypeStruct((rows, 2 * width), BF16),) * nj,
        in_specs=[smem] + [vmem] * 4,
        out_specs=(vmem,) * (nx + nj),
        scratch_shapes=[
            pltpu.VMEM((2, 2, width, nx * rows), F32),
            pltpu.VMEM((2, 1, nx * rows), F32),
            pltpu.VMEM((2, 1, nx * rows), F32),
            pltpu.VMEM((2, *kv.shape), F32),
            pltpu.VMEM((2, 2 * nx, rows), F32),
        ],
        compiler_params=pltpu.CompilerParams(vmem_limit_bytes=VMEM),
        cost_estimate=pl.CostEstimate(flops=10 * pairs, bytes_accessed=2 << 20, transcendentals=0),
        name="backward",
    )(where, all_q, all_g, kv, got)
    parts, dkv = both[:nx], both[nx:]
    parts = [parts[0]] + [shifted(parts[-r % nx], "x", nx, r) for r in range(1, nx)]
    dkv = [dkv[0]] + [shifted(dkv[r], "zj", nj, r) for r in range(1, nj)]
    near, far = pl.pallas_call(
        functools.partial(mix_kernel, nx),
        out_shape=(
            jax.ShapeDtypeStruct((width, rows), F32),
            jax.ShapeDtypeStruct((width, rows), BF16),
        ),
        in_specs=[smem] + [vmem] * (nx + 1),
        out_specs=(vmem,) * 2,
        compiler_params=pltpu.CompilerParams(vmem_limit_bytes=8 << 20),
        name="mix",
    )(where, got, *offers)
    back = functools.reduce(jnp.add, [p[:, rows:].astype(F32) for p in parts]).astype(BF16)
    back = swapped(jnp.concatenate([back, far], axis=1), nz)
    return pl.pallas_call(
        functools.partial(final_kernel, nx, nj),
        out_shape=(jax.ShapeDtypeStruct((rows, width), BF16),)
        + (jax.ShapeDtypeStruct((rows, width), F32),) * 3,
        in_specs=[vmem] * (nx + nj + 2),
        out_specs=(vmem,) * 4,
        compiler_params=pltpu.CompilerParams(vmem_limit_bytes=8 << 20),
        name="final",
    )(*parts, near, back, *dkv)


def solution(mesh):
    nh = mesh.shape["head"]
    split = Mesh(mesh.devices.reshape(4, 2, -1, nh), (*SEQ, "head"))
    return jax.shard_map(
        functools.partial(per_device, 4, split.shape["x"], nh),
        mesh=split,
        in_specs=(P(SEQ, "head"), P((*SEQ, "head"), None), P((*SEQ, "head"), None), P(SEQ, "head")),
        out_specs=(P(SEQ, "head"),) * 4,
        check_vma=False,
    )
```

time: 90.1 us -> 87.8 us (0.974)
  blocking collectives: 15.1 us -> 0 us
  starting transfers between devices: 36.1 us -> 45.9 us
  waiting for transfers between devices: 23.4 us -> 26.3 us
    all_to_all x1 -> x0, blocking collectives: 15.1 us -> none  [per_device(): got = lax.all_to_all(parts, SEQ, 0, 0, axis_index_groups=groups, tiled=True)]
    ppermute x12 -> x15, starting transfers between devices: 20.7 us -> 25.7 us  [shifted(): lax.ppermute(value, axis, [(i, (i + step) % count) for i in range(count)])]
    all_to_all x0 -> x1, starting transfers between devices: none -> 4.75 us  [per_device(): got = lax.all_to_all(sent, SEQ, 0, 0, axis_index_groups=groups, tiled=True)]
    ppermute x12 -> x15, waiting for transfers between devices: 12.8 us -> 14.3 us  [shifted(): lax.ppermute(value, axis, [(i, (i + step) % count) for i in range(count)])]
    ppermute x2, waiting for transfers between devices: 10.6 us -> 11.8 us  [swapped(): return lax.ppermute(value, Z, pairs + [(j, i) for i, j in pairs])]
  transfers between devices with their start and end apart: 15 -> 19, of which waited for: 7 -> 9; matrix products, arithmetic and copies ran while one was open for 0% -> 0% of each run, Pallas kernels for 2% -> 7%
where the time goes in v1:
time: 87.8 us; the launch traced here: 86.4 us
  starting transfers between devices  45.9 us (52%)
  waiting for transfers between devices  26.3 us (30%)
  Pallas kernels  13.4 us (15%)
    ppermute x15, starting transfers between devices, shifted(): lax.ppermute(value, axis, [(i, (i + step) % count) for i in range(count)])  25.7 us
    ppermute x15, waiting for transfers between devices, shifted(): lax.ppermute(value, axis, [(i, (i + step) % count) for i in range(count)])  14.3 us
    all_to_all x1, starting transfers between devices, per_device(): kv = lax.all_to_all(mixed, ('zj', 'head'), 0, 0, tiled=True)  11.8 us
    ppermute x2, waiting for transfers between devices, swapped(): return lax.ppermute(value, Z, pairs + [(j, i) for i, j in pairs])  11.8 us
    pallas_call x1, Pallas kernels, per_device(): pl.pallas_call(functools.partial(backward_kernel, rate, scaling, nx), out...  5.16 us
    pallas_call x1, Pallas kernels, per_device(): pl.pallas_call(functools.partial(forward_kernel, rate, nx), out_shape=(ja...  4.77 us
    all_to_all x1, starting transfers between devices, per_device(): got = lax.all_to_all(sent, SEQ, 0, 0, axis_index_groups=groups, tiled=True)  4.75 us
    ppermute x2, starting transfers between devices, swapped(): return lax.ppermute(value, Z, pairs + [(j, i) for i, j in pairs])  3.62 us
  transfers between devices with their start and end apart: 19, of which 9 were waited for; matrix products, arithmetic and copies ran while one was open for 0% of the time, Pallas kernels for 7%

profile of v1, /device:TPU:8, one launch (start us, length us, event | category | flops | bytes accessed | tf_op | source)
XLA Modules:
  0.0 86.4 jit_solution(4420587049192369267)
XLA Ops:
  0.6 1.8 %prepare.1 = (bf16[256,256]{1,0:T(8,128)(2,1)}, bf16[32,32,256]{2,1,0:T(8,128)(2,1)}) custom-call(bf16[256,128]{1,0:T(8,128)(2,1)} %refs_0_.1, bf16[256,128]{1,0:T(8,128)(2,1)} %refs_1_.1, bf16[32,1024]{1,0:T(8,128)(2,1)} %k_ref.1, bf16[32,1024]{1,0:T(8,128)(2,1)} %v_ref.1), custom_call_target="tpu_custom_call" | custom-call | tf_op jit(solution)/shard_map/prepare/pallas_call | solution.py:245
  2.5 0.0 copy-start.2
  2.5 0.0 copy-start
  2.5 0.0 copy-start.1
  2.5 11.8 %all-to-all-start = ((bf16[32,32,256]{2,1,0:T(8,128)(2,1)}), bf16[32,32,256]{2,1,0:T(8,128)(2,1)S(1)}, u32[]{:S(2)}, u32[]{:S(2)}) async-start(bf16[32,32,256]{2,1,0:T(8,128)(2,1)} %get-tuple-element.24), calls=%async_computation | async-start | bytes 1048576 | tf_op jit(solution)/shard_map/all_to_all | solution.py:261
  14.3 0.0 copy-done.2
  14.4 3.3 %collective-permute-start.3 = (bf16[256,256]{1,0:T(8,128)(2,1)S(1)}, bf16[256,256]{1,0:T(8,128)(2,1)S(1)}, u32[]{:S(2)}, u32[]{:S(2)}) collective-permute-start(bf16[256,256]{1,0:T(8,128)(2,1)S(1)} %copy-done.2), channel_id=1, source_target_pairs={{32,64},{96,128},{160,192},{224,0},{64,32},{128,96},{192,160},{0,2... | collective-permute-start | bytes 393224 | tf_op jit(solution)/shard_map/ppermute | solution.py:235
  17.6 2.8 %collective-permute-start.2 = (bf16[256,256]{1,0:T(8,128)(2,1)S(1)}, bf16[256,256]{1,0:T(8,128)(2,1)S(1)}, u32[]{:S(2)}, u32[]{:S(2)}) collective-permute-start(bf16[256,256]{1,0:T(8,128)(2,1)S(1)} %copy-done.2), channel_id=1, source_target_pairs={{0,24},{8,0},{16,8},{24,16},{1,25},{9,1},{17,9},{25,17},{2,26},{10... | collective-permute-start | bytes 393224 | tf_op jit(solution)/shard_map/ppermute | solution.py:230
  20.4 0.8 collective-permute-start.1
  21.2 0.9 %collective-permute-start = (bf16[256,256]{1,0:T(8,128)(2,1)S(1)}, bf16[256,256]{1,0:T(8,128)(2,1)S(1)}, u32[]{:S(2)}, u32[]{:S(2)}) collective-permute-start(bf16[256,256]{1,0:T(8,128)(2,1)S(1)} %copy-done.2), channel_id=1, source_target_pairs={{0,8},{8,16},{16,24},{24,0},{1,9},{9,17},{17,25},{25,1},{2,10},{10... | collective-permute-start | bytes 393224 | tf_op jit(solution)/shard_map/ppermute | solution.py:230
  22.1 10.6 %collective-permute-done.3.refs_5_ = bf16[256,256]{1,0:T(8,128)(2,1)S(1)} collective-permute-done((bf16[256,256]{1,0:T(8,128)(2,1)S(1)}, bf16[256,256]{1,0:T(8,128)(2,1)S(1)}, u32[]{:S(2)}, u32[]{:S(2)}) %collective-permute-start.3) | collective-permute-done | bytes 131104 | tf_op jit(solution)/shard_map/ppermute | solution.py:235
  32.6 2.8 %collective-permute-start.6 = (bf16[256,256]{1,0:T(8,128)(2,1)S(1)}, bf16[256,256]{1,0:T(8,128)(2,1)S(1)}, u32[]{:S(2)}, u32[]{:S(2)}) collective-permute-start(bf16[256,256]{1,0:T(8,128)(2,1)S(1)} %collective-permute-done.3.refs_5_), channel_id=1, source_target_pairs={{0,24},{8,0},{16,8},{24,16},{1,25},{9,1},{17,9},{25,17},{2,26},{10... | collective-permute-start | bytes 393224 | tf_op jit(solution)/shard_map/ppermute | solution.py:230
  35.4 0.8 collective-permute-start.5
  36.2 0.0 collective-permute-done.2.refs_4_
  36.2 0.9 %collective-permute-start.4 = (bf16[256,256]{1,0:T(8,128)(2,1)S(1)}, bf16[256,256]{1,0:T(8,128)(2,1)S(1)}, u32[]{:S(2)}, u32[]{:S(2)}) collective-permute-start(bf16[256,256]{1,0:T(8,128)(2,1)S(1)} %collective-permute-done.3.refs_5_), channel_id=1, source_target_pairs={{0,8},{8,16},{16,24},{24,0},{1,9},{9,17},{17,25},{25,1},{2,10},{10... | collective-permute-start | bytes 393224 | tf_op jit(solution)/shard_map/ppermute | solution.py:230
  37.1 0.1 pad_add_fusion.where_ref
  37.2 0.0 collective-permute-done.1.refs_3_
  37.2 0.0 collective-permute-done.refs_2_
  37.2 3.6 %collective-permute-done.6.refs_8_ = bf16[256,256]{1,0:T(8,128)(2,1)S(1)} collective-permute-done((bf16[256,256]{1,0:T(8,128)(2,1)S(1)}, bf16[256,256]{1,0:T(8,128)(2,1)S(1)}, u32[]{:S(2)}, u32[]{:S(2)}) %collective-permute-start.6) | collective-permute-done | bytes 131104 | tf_op jit(solution)/shard_map/ppermute | solution.py:230
  40.7 2.3 %collective-permute-done.5.refs_7_ = bf16[256,256]{1,0:T(8,128)(2,1)S(1)} collective-permute-done((bf16[256,256]{1,0:T(8,128)(2,1)S(1)}, bf16[256,256]{1,0:T(8,128)(2,1)S(1)}, u32[]{:S(2)}, u32[]{:S(2)}) %collective-permute-start.5) | collective-permute-done | bytes 131104 | tf_op jit(solution)/shard_map/ppermute | solution.py:230
  43.0 1.4 %collective-permute-done.4.refs_6_ = bf16[256,256]{1,0:T(8,128)(2,1)S(1)} collective-permute-done((bf16[256,256]{1,0:T(8,128)(2,1)S(1)}, bf16[256,256]{1,0:T(8,128)(2,1)S(1)}, u32[]{:S(2)}, u32[]{:S(2)}) %collective-permute-start.4) | collective-permute-done | bytes 131104 | tf_op jit(solution)/shard_map/ppermute | solution.py:230
  44.4 0.0 all-to-all-done
  44.4 0.0 copy-done
  44.4 0.0 copy-done.1
  44.4 4.8 %forward.1 = (bf16[128,512]{1,0:T(8,128)(2,1)S(1)}, bf16[128,512]{1,0:T(8,128)(2,1)S(1)}, bf16[128,512]{1,0:T(8,128)(2,1)S(1)}, bf16[128,512]{1,0:T(8,128)(2,1)S...) custom-call(s32[4]{0:T(128)S(1)} %pad_add_fusion.where_ref, ...), custom_call_target="tpu_custom_call" | custom-call | flops 939524096 | bytes 2097152 | tf_op jit(solution)/shard_map/forward/pallas_call | solution.py:271
  49.2 4.8 %all-to-all-start.1 = ((f32[8,24,256]{2,1,0:T(8,128)}), f32[8,24,256]{2,1,0:T(8,128)S(1)}, u32[]{:S(2)}, u32[]{:S(2)}) async-start(f32[8,24,256]{2,1,0:T(8,128)} %get-tuple-element.27), calls=%async_computation.1 | async-start | bytes 393216 | tf_op jit(solution)/shard_map/all_to_all | solution.py:291
  54.0 1.5 %collective-permute-start.10 = (bf16[128,512]{1,0:T(8,128)(2,1)S(1)}, bf16[128,512]{1,0:T(8,128)(2,1)S(1)}, u32[]{:S(2)}, u32[]{:S(2)}) collective-permute-start(bf16[128,512]{1,0:T(8,128)(2,1)S(1)} %get-tuple-element.33), channel_id=1, source_target_pairs={{0,8},{8,16},{16,24},{24,0},{1,9},{9,17},{17,25},{25,1},{2,10},{10... | collective-permute-start | bytes 393224 | tf_op jit(solution)/shard_map/ppermute | solution.py:230
  55.4 2.7 %collective-permute-start.11 = (bf16[128,512]{1,0:T(8,128)(2,1)S(1)}, bf16[128,512]{1,0:T(8,128)(2,1)S(1)}, u32[]{:S(2)}, u32[]{:S(2)}) collective-permute-start(bf16[128,512]{1,0:T(8,128)(2,1)S(1)} %get-tuple-element.34), channel_id=1, source_target_pairs={{0,16},{8,24},{16,0},{24,8},{1,17},{9,25},{17,1},{25,9},{2,18},{10... | collective-permute-start | bytes 393224 | tf_op jit(solution)/shard_map/ppermute | solution.py:230
  58.1 1.5 %collective-permute-start.12 = (bf16[128,512]{1,0:T(8,128)(2,1)S(1)}, bf16[128,512]{1,0:T(8,128)(2,1)S(1)}, u32[]{:S(2)}, u32[]{:S(2)}) collective-permute-start(bf16[128,512]{1,0:T(8,128)(2,1)S(1)} %get-tuple-element.35), channel_id=1, source_target_pairs={{0,24},{8,0},{16,8},{24,16},{1,25},{9,1},{17,9},{25,17},{2,26},{10... | collective-permute-start | bytes 393224 | tf_op jit(solution)/shard_map/ppermute | solution.py:230
  59.6 0.2 all-to-all-done.1.refs_3_.got_ref
  59.7 5.2 %backward.1 = (bf16[128,512]{1,0:T(8,128)(2,1)S(1)}, bf16[128,512]{1,0:T(8,128)(2,1)S(1)}, bf16[128,512]{1,0:T(8,128)(2,1)S(1)}, bf16[128,512]{1,0:T(8,128)(2,1)...) custom-call(s32[4]{0:T(128)S(1)} %pad_add_fusion.where_ref, ...), custom_call_target="tpu_custom_call" | custom-call | flops 2348810240 | bytes 2097152 | tf_op jit(solution)/shard_map/backward/pallas_call | solution.py:293
  64.9 1.1 %collective-permute-start.7 = (bf16[128,512]{1,0:T(8,128)(2,1)S(1)}, bf16[128,512]{1,0:T(8,128)(2,1)S(1)}, u32[]{:S(2)}, u32[]{:S(2)}) collective-permute-start(bf16[128,512]{1,0:T(8,128)(2,1)S(1)} %get-tuple-element.29), channel_id=1, source_target_pairs={{0,8},{8,16},{16,24},{24,0},{1,9},{9,17},{17,25},{25,1},{2,10},{10... | collective-permute-start | bytes 393224 | tf_op jit(solution)/shard_map/ppermute | solution.py:230
  66.0 2.1 %collective-permute-start.8 = (bf16[128,512]{1,0:T(8,128)(2,1)S(1)}, bf16[128,512]{1,0:T(8,128)(2,1)S(1)}, u32[]{:S(2)}, u32[]{:S(2)}) collective-permute-start(bf16[128,512]{1,0:T(8,128)(2,1)S(1)} %get-tuple-element.30), channel_id=1, source_target_pairs={{0,16},{8,24},{16,0},{24,8},{1,17},{9,25},{17,1},{25,9},{2,18},{10... | collective-permute-start | bytes 393224 | tf_op jit(solution)/shard_map/ppermute | solution.py:230
  68.1 0.0 collective-permute-done.10.refs_1_
  68.1 0.7 collective-permute-start.9
  68.8 0.0 collective-permute-done.11.refs_2_
  68.8 0.0 collective-permute-start.14
  68.8 0.0 collective-permute-done.12.refs_3_
  68.8 5.9 %collective-permute-start.15 = (bf16[256,256]{1,0:T(8,128)(2,1)S(1)}, bf16[256,256]{1,0:T(8,128)(2,1)S(1)}, u32[]{:S(2)}, u32[]{:S(2)}) collective-permute-start(bf16[256,256]{1,0:T(8,128)(2,1)S(1)} %get-tuple-element.40), channel_id=1, source_target_pairs={{0,128},{64,192},{128,0},{192,64},{1,129},{65,193},{129,1},{193,65... | collective-permute-start | bytes 393224 | tf_op jit(solution)/shard_map/ppermute | solution.py:230
  74.8 0.7 mix.1
  75.5 0.0 collective-permute-done.7.refs_1_
  75.5 1.4 %collective-permute-start.16 = (bf16[256,256]{1,0:T(8,128)(2,1)S(1)}, bf16[256,256]{1,0:T(8,128)(2,1)S(1)}, u32[]{:S(2)}, u32[]{:S(2)}) collective-permute-start(bf16[256,256]{1,0:T(8,128)(2,1)S(1)} %get-tuple-element.41), channel_id=1, source_target_pairs={{0,192},{64,0},{128,64},{192,128},{1,193},{65,1},{129,65},{193,129... | collective-permute-start | bytes 393224 | tf_op jit(solution)/shard_map/ppermute | solution.py:230
  76.8 0.0 collective-permute-done.8.refs_2_
  76.8 0.0 collective-permute-done.9.refs_3_
  76.9 0.3 collective-permute-start.13
  77.3 2.3 %collective-permute-done.14.refs_7_ = bf16[256,256]{1,0:T(8,128)(2,1)S(1)} collective-permute-done((bf16[256,256]{1,0:T(8,128)(2,1)S(1)}, bf16[256,256]{1,0:T(8,128)(2,1)S(1)}, u32[]{:S(2)}, u32[]{:S(2)}) %collective-permute-start.14) | collective-permute-done | bytes 131104 | tf_op jit(solution)/shard_map/ppermute | solution.py:230
  79.6 2.6 %collective-permute-done.15.refs_8_ = bf16[256,256]{1,0:T(8,128)(2,1)S(1)} collective-permute-done((bf16[256,256]{1,0:T(8,128)(2,1)S(1)}, bf16[256,256]{1,0:T(8,128)(2,1)S(1)}, u32[]{:S(2)}, u32[]{:S(2)}) %collective-permute-start.15) | collective-permute-done | bytes 131104 | tf_op jit(solution)/shard_map/ppermute | solution.py:230
  82.1 2.2 %collective-permute-done.16.refs_9_ = bf16[256,256]{1,0:T(8,128)(2,1)S(1)} collective-permute-done((bf16[256,256]{1,0:T(8,128)(2,1)S(1)}, bf16[256,256]{1,0:T(8,128)(2,1)S(1)}, u32[]{:S(2)}, u32[]{:S(2)}) %collective-permute-start.16) | collective-permute-done | bytes 131104 | tf_op jit(solution)/shard_map/ppermute | solution.py:230
  84.3 1.2 %collective-permute-done.13.refs_5_ = bf16[128,512]{1,0:T(8,128)(2,1)S(1)} collective-permute-done((bf16[128,512]{1,0:T(8,128)(2,1)S(1)}, bf16[128,512]{1,0:T(8,128)(2,1)S(1)}, u32[]{:S(2)}, u32[]{:S(2)}) %collective-permute-start.13) | collective-permute-done | bytes 131104 | tf_op jit(solution)/shard_map/ppermute | solution.py:235
  85.5 0.9 %final.1 = (bf16[256,128]{1,0:T(8,128)(2,1)}, f32[256,128]{1,0:T(8,128)}, f32[256,128]{1,0:T(8,128)}, f32[256,128]{1,0:T(8,128)}) custom-call(bf16[128,512]{1,0:T(8,128)(2,1)S(1)} %get-tuple-element.28.refs_0_, bf16[128,512]{1,0:T(8,128)(2,1)S(1)} %collective-permute-done.7.refs_1_, bf16[128,512]{1,0:T(8,128)(2,1)S(1)} %collective-permute-done.8.refs_2_, ...), custom_call_target="tpu_custom_call" | custom-call | tf_op jit(solution)/shard_map/final/pallas_call | solution.py:326
  (2 shorter events, 0.0 us)
Async XLA Ops:
  2.5 11.9 %copy-start.2 = (bf16[256,256]{1,0:T(8,128)(2,1)S(1)}, bf16[256,256]{1,0:T(8,128)(2,1)}, u32[]{:S(2)}) copy-start(bf16[256,256]{1,0:T(8,128)(2,1)} %get-tuple-element.23) | copy-start | bytes 393220
  2.5 41.9 %copy-start = (bf16[256,128]{1,0:T(8,128)(2,1)S(1)}, bf16[256,128]{1,0:T(8,128)(2,1)}, u32[]{:S(2)}) copy-start(bf16[256,128]{1,0:T(8,128)(2,1)} %refs_0_.1) | copy-start | bytes 196612
  2.5 41.9 %copy-start.1 = (bf16[256,128]{1,0:T(8,128)(2,1)S(1)}, bf16[256,128]{1,0:T(8,128)(2,1)}, u32[]{:S(2)}) copy-start(bf16[256,128]{1,0:T(8,128)(2,1)} %refs_1_.1) | copy-start | bytes 196612
  2.5 41.9 %all-to-all-start = ((bf16[32,32,256]{2,1,0:T(8,128)(2,1)}), bf16[32,32,256]{2,1,0:T(8,128)(2,1)S(1)}, u32[]{:S(2)}, u32[]{:S(2)}) async-start(bf16[32,32,256]{2,1,0:T(8,128)(2,1)} %get-tuple-element.24), calls=%async_computation | async-start | bytes 1048576 | tf_op jit(solution)/shard_map/all_to_all | solution.py:261
  14.4 18.3 %collective-permute-start.3 = (bf16[256,256]{1,0:T(8,128)(2,1)S(1)}, bf16[256,256]{1,0:T(8,128)(2,1)S(1)}, u32[]{:S(2)}, u32[]{:S(2)}) collective-permute-start(bf16[256,256]{1,0:T(8,128)(2,1)S(1)} %copy-done.2), channel_id=1, source_target_pairs={{32,64},{96,128},{160,192},{224,0},{64,32},{128,96},{192,160},{0,2... | collective-permute-start | bytes 393224 | tf_op jit(solution)/shard_map/ppermute | solution.py:235
  17.6 18.6 %collective-permute-start.2 = (bf16[256,256]{1,0:T(8,128)(2,1)S(1)}, bf16[256,256]{1,0:T(8,128)(2,1)S(1)}, u32[]{:S(2)}, u32[]{:S(2)}) collective-permute-start(bf16[256,256]{1,0:T(8,128)(2,1)S(1)} %copy-done.2), channel_id=1, source_target_pairs={{0,24},{8,0},{16,8},{24,16},{1,25},{9,1},{17,9},{25,17},{2,26},{10... | collective-permute-start | bytes 393224 | tf_op jit(solution)/shard_map/ppermute | solution.py:230
  20.4 16.8 %collective-permute-start.1 = (bf16[256,256]{1,0:T(8,128)(2,1)S(1)}, bf16[256,256]{1,0:T(8,128)(2,1)S(1)}, u32[]{:S(2)}, u32[]{:S(2)}) collective-permute-start(bf16[256,256]{1,0:T(8,128)(2,1)S(1)} %copy-done.2), channel_id=1, source_target_pairs={{0,16},{8,24},{16,0},{24,8},{1,17},{9,25},{17,1},{25,9},{2,18},{10... | collective-permute-start | bytes 393224 | tf_op jit(solution)/shard_map/ppermute | solution.py:230
  21.2 16.0 %collective-permute-start = (bf16[256,256]{1,0:T(8,128)(2,1)S(1)}, bf16[256,256]{1,0:T(8,128)(2,1)S(1)}, u32[]{:S(2)}, u32[]{:S(2)}) collective-permute-start(bf16[256,256]{1,0:T(8,128)(2,1)S(1)} %copy-done.2), channel_id=1, source_target_pairs={{0,8},{8,16},{16,24},{24,0},{1,9},{9,17},{17,25},{25,1},{2,10},{10... | collective-permute-start | bytes 393224 | tf_op jit(solution)/shard_map/ppermute | solution.py:230
  32.6 8.1 %collective-permute-start.6 = (bf16[256,256]{1,0:T(8,128)(2,1)S(1)}, bf16[256,256]{1,0:T(8,128)(2,1)S(1)}, u32[]{:S(2)}, u32[]{:S(2)}) collective-permute-start(bf16[256,256]{1,0:T(8,128)(2,1)S(1)} %collective-permute-done.3.refs_5_), channel_id=1, source_target_pairs={{0,24},{8,0},{16,8},{24,16},{1,25},{9,1},{17,9},{25,17},{2,26},{10... | collective-permute-start | bytes 393224 | tf_op jit(solution)/shard_map/ppermute | solution.py:230
  35.4 7.6 %collective-permute-start.5 = (bf16[256,256]{1,0:T(8,128)(2,1)S(1)}, bf16[256,256]{1,0:T(8,128)(2,1)S(1)}, u32[]{:S(2)}, u32[]{:S(2)}) collective-permute-start(bf16[256,256]{1,0:T(8,128)(2,1)S(1)} %collective-permute-done.3.refs_5_), channel_id=1, source_target_pairs={{0,16},{8,24},{16,0},{24,8},{1,17},{9,25},{17,1},{25,9},{2,18},{10... | collective-permute-start | bytes 393224 | tf_op jit(solution)/shard_map/ppermute | solution.py:230
  36.2 8.2 %collective-permute-start.4 = (bf16[256,256]{1,0:T(8,128)(2,1)S(1)}, bf16[256,256]{1,0:T(8,128)(2,1)S(1)}, u32[]{:S(2)}, u32[]{:S(2)}) collective-permute-start(bf16[256,256]{1,0:T(8,128)(2,1)S(1)} %collective-permute-done.3.refs_5_), channel_id=1, source_target_pairs={{0,8},{8,16},{16,24},{24,0},{1,9},{9,17},{17,25},{25,1},{2,10},{10... | collective-permute-start | bytes 393224 | tf_op jit(solution)/shard_map/ppermute | solution.py:230
  49.2 10.5 %all-to-all-start.1 = ((f32[8,24,256]{2,1,0:T(8,128)}), f32[8,24,256]{2,1,0:T(8,128)S(1)}, u32[]{:S(2)}, u32[]{:S(2)}) async-start(f32[8,24,256]{2,1,0:T(8,128)} %get-tuple-element.27), calls=%async_computation.1 | async-start | bytes 393216 | tf_op jit(solution)/shard_map/all_to_all | solution.py:291
  54.0 14.2 %collective-permute-start.10 = (bf16[128,512]{1,0:T(8,128)(2,1)S(1)}, bf16[128,512]{1,0:T(8,128)(2,1)S(1)}, u32[]{:S(2)}, u32[]{:S(2)}) collective-permute-start(bf16[128,512]{1,0:T(8,128)(2,1)S(1)} %get-tuple-element.33), channel_id=1, source_target_pairs={{0,8},{8,16},{16,24},{24,0},{1,9},{9,17},{17,25},{25,1},{2,10},{10... | collective-permute-start | bytes 393224 | tf_op jit(solution)/shard_map/ppermute | solution.py:230
  55.4 13.4 %collective-permute-start.11 = (bf16[128,512]{1,0:T(8,128)(2,1)S(1)}, bf16[128,512]{1,0:T(8,128)(2,1)S(1)}, u32[]{:S(2)}, u32[]{:S(2)}) collective-permute-start(bf16[128,512]{1,0:T(8,128)(2,1)S(1)} %get-tuple-element.34), channel_id=1, source_target_pairs={{0,16},{8,24},{16,0},{24,8},{1,17},{9,25},{17,1},{25,9},{2,18},{10... | collective-permute-start | bytes 393224 | tf_op jit(solution)/shard_map/ppermute | solution.py:230
  58.1 10.7 %collective-permute-start.12 = (bf16[128,512]{1,0:T(8,128)(2,1)S(1)}, bf16[128,512]{1,0:T(8,128)(2,1)S(1)}, u32[]{:S(2)}, u32[]{:S(2)}) collective-permute-start(bf16[128,512]{1,0:T(8,128)(2,1)S(1)} %get-tuple-element.35), channel_id=1, source_target_pairs={{0,24},{8,0},{16,8},{24,16},{1,25},{9,1},{17,9},{25,17},{2,26},{10... | collective-permute-start | bytes 393224 | tf_op jit(solution)/shard_map/ppermute | solution.py:230
  64.9 10.6 %collective-permute-start.7 = (bf16[128,512]{1,0:T(8,128)(2,1)S(1)}, bf16[128,512]{1,0:T(8,128)(2,1)S(1)}, u32[]{:S(2)}, u32[]{:S(2)}) collective-permute-start(bf16[128,512]{1,0:T(8,128)(2,1)S(1)} %get-tuple-element.29), channel_id=1, source_target_pairs={{0,8},{8,16},{16,24},{24,0},{1,9},{9,17},{17,25},{25,1},{2,10},{10... | collective-permute-start | bytes 393224 | tf_op jit(solution)/shard_map/ppermute | solution.py:230
  66.0 10.8 %collective-permute-start.8 = (bf16[128,512]{1,0:T(8,128)(2,1)S(1)}, bf16[128,512]{1,0:T(8,128)(2,1)S(1)}, u32[]{:S(2)}, u32[]{:S(2)}) collective-permute-start(bf16[128,512]{1,0:T(8,128)(2,1)S(1)} %get-tuple-element.30), channel_id=1, source_target_pairs={{0,16},{8,24},{16,0},{24,8},{1,17},{9,25},{17,1},{25,9},{2,18},{10... | collective-permute-start | bytes 393224 | tf_op jit(solution)/shard_map/ppermute | solution.py:230
  68.1 8.7 %collective-permute-start.9 = (bf16[128,512]{1,0:T(8,128)(2,1)S(1)}, bf16[128,512]{1,0:T(8,128)(2,1)S(1)}, u32[]{:S(2)}, u32[]{:S(2)}) collective-permute-start(bf16[128,512]{1,0:T(8,128)(2,1)S(1)} %get-tuple-element.31), channel_id=1, source_target_pairs={{0,24},{8,0},{16,8},{24,16},{1,25},{9,1},{17,9},{25,17},{2,26},{10... | collective-permute-start | bytes 393224 | tf_op jit(solution)/shard_map/ppermute | solution.py:230
  68.8 10.7 %collective-permute-start.14 = (bf16[256,256]{1,0:T(8,128)(2,1)S(1)}, bf16[256,256]{1,0:T(8,128)(2,1)S(1)}, u32[]{:S(2)}, u32[]{:S(2)}) collective-permute-start(bf16[256,256]{1,0:T(8,128)(2,1)S(1)} %get-tuple-element.39), channel_id=1, source_target_pairs={{0,64},{64,128},{128,192},{192,0},{1,65},{65,129},{129,193},{193,1... | collective-permute-start | bytes 393224 | tf_op jit(solution)/shard_map/ppermute | solution.py:230
  68.8 13.3 %collective-permute-start.15 = (bf16[256,256]{1,0:T(8,128)(2,1)S(1)}, bf16[256,256]{1,0:T(8,128)(2,1)S(1)}, u32[]{:S(2)}, u32[]{:S(2)}) collective-permute-start(bf16[256,256]{1,0:T(8,128)(2,1)S(1)} %get-tuple-element.40), channel_id=1, source_target_pairs={{0,128},{64,192},{128,0},{192,64},{1,129},{65,193},{129,1},{193,65... | collective-permute-start | bytes 393224 | tf_op jit(solution)/shard_map/ppermute | solution.py:230
  75.5 8.8 %collective-permute-start.16 = (bf16[256,256]{1,0:T(8,128)(2,1)S(1)}, bf16[256,256]{1,0:T(8,128)(2,1)S(1)}, u32[]{:S(2)}, u32[]{:S(2)}) collective-permute-start(bf16[256,256]{1,0:T(8,128)(2,1)S(1)} %get-tuple-element.41), channel_id=1, source_target_pairs={{0,192},{64,0},{128,64},{192,128},{1,193},{65,1},{129,65},{193,129... | collective-permute-start | bytes 393224 | tf_op jit(solution)/shard_map/ppermute | solution.py:230
  76.9 8.6 %collective-permute-start.13 = (bf16[128,512]{1,0:T(8,128)(2,1)S(1)}, bf16[128,512]{1,0:T(8,128)(2,1)S(1)}, u32[]{:S(2)}, u32[]{:S(2)}) collective-permute-start(bf16[128,512]{1,0:T(8,128)(2,1)S(1)} %pad_maximum_fusion), channel_id=1, source_target_pairs={{32,64},{96,128},{160,192},{224,0},{64,32},{128,96},{192,160},{0,2... | collective-permute-start | bytes 393224 | tf_op jit(solution)/shard_map/ppermute | solution.py:235

commit v2 on v1

--- a/solution.py
+++ b/solution.py
@@ -233,6 +233,11 @@
 def swapped(value, count):
     pairs = [(i, (i + 1) % count) for i in range(1, count, 2)]
     return lax.ppermute(value, Z, pairs + [(j, i) for i, j in pairs])
+
+
+def worked(nj, step):
+    steps = [(a, (a + step) % nj, p) for a in range(nj) for p in range(2)]
+    return [(2 * a + p, 2 * b + p) for a, b, p in steps if b <= a or a == p == 0]
 
 
 def per_device(nj, nx, nh, queries, keys, values, out_grad):
@@ -309,7 +314,7 @@
     )(where, all_q, all_g, kv, got)
     parts, dkv = both[:nx], both[nx:]
     parts = [parts[0]] + [shifted(parts[-r % nx], "x", nx, r) for r in range(1, nx)]
-    dkv = [dkv[0]] + [shifted(dkv[r], "zj", nj, r) for r in range(1, nj)]
+    dkv = [dkv[0]] + [lax.ppermute(dkv[r], Z, worked(nj, r)) for r in range(1, nj)]
     near, far = pl.pallas_call(
         functools.partial(mix_kernel, nx),
         out_shape=(

time: 87.8 us -> 86.6 us (0.986); the launches traced: 86.4 us -> 86.1 us
  waiting for transfers between devices: 26.3 us -> 24.2 us
  starting transfers between devices: 45.9 us -> 47.6 us
    ppermute x0 -> x3, starting transfers between devices: none -> 9.24 us  [per_device(): lax.ppermute(dkv[r], Z, worked(nj, r))]
    ppermute x15 -> x12, starting transfers between devices: 25.7 us -> 18.4 us  [shifted(): lax.ppermute(value, axis, [(i, (i + step) % count) for i in range(count)])]
    ppermute x15 -> x12, waiting for transfers between devices: 14.3 us -> 7.26 us  [shifted(): lax.ppermute(value, axis, [(i, (i + step) % count) for i in range(count)])]
    ppermute x0 -> x3, waiting for transfers between devices: none -> 5.29 us  [per_device(): lax.ppermute(dkv[r], Z, worked(nj, r))]
where the time goes in v2:
time: 86.6 us; the launch traced here: 86.1 us
  starting transfers between devices  47.6 us (55%)
  waiting for transfers between devices  24.2 us (28%)
  Pallas kernels  13.4 us (15%)
    ppermute x12, starting transfers between devices, shifted(): lax.ppermute(value, axis, [(i, (i + step) % count) for i in range(count)])  18.4 us
    all_to_all x1, starting transfers between devices, per_device(): kv = lax.all_to_all(mixed, ('zj', 'head'), 0, 0, tiled=True)  11.8 us
    ppermute x2, waiting for transfers between devices, swapped(): return lax.ppermute(value, Z, pairs + [(j, i) for i, j in pairs])  11.5 us
    ppermute x3, starting transfers between devices, per_device(): lax.ppermute(dkv[r], Z, worked(nj, r))  9.24 us
    ppermute x12, waiting for transfers between devices, shifted(): lax.ppermute(value, axis, [(i, (i + step) % count) for i in range(count)])  7.26 us
    ppermute x3, waiting for transfers between devices, per_device(): lax.ppermute(dkv[r], Z, worked(nj, r))  5.29 us
    pallas_call x1, Pallas kernels, per_device(): pl.pallas_call(functools.partial(backward_kernel, rate, scaling, nx), out...  5.16 us
    pallas_call x1, Pallas kernels, per_device(): pl.pallas_call(functools.partial(forward_kernel, rate, nx), out_shape=(ja...  4.77 us
  transfers between devices with their start and end apart: 19, of which 9 were waited for; matrix products, arithmetic and copies ran while one was open for 0% of the time, Pallas kernels for 7%

profile of v2, /device:TPU:8, one launch (start us, length us, event | category | flops | bytes accessed | tf_op | source)
XLA Modules:
  0.0 86.1 jit_solution(1298994682570809022)
XLA Ops:
  0.6 1.8 %prepare.1 = (bf16[256,256]{1,0:T(8,128)(2,1)}, bf16[32,32,256]{2,1,0:T(8,128)(2,1)}) custom-call(bf16[256,128]{1,0:T(8,128)(2,1)} %refs_0_.1, bf16[256,128]{1,0:T(8,128)(2,1)} %refs_1_.1, bf16[32,1024]{1,0:T(8,128)(2,1)} %k_ref.1, bf16[32,1024]{1,0:T(8,128)(2,1)} %v_ref.1), custom_call_target="tpu_custom_call" | custom-call | tf_op jit(solution)/shard_map/prepare/pallas_call | solution.py:250
  2.5 0.0 copy-start.2
  2.5 0.0 copy-start
  2.5 0.0 copy-start.1
  2.5 11.8 %all-to-all-start = ((bf16[32,32,256]{2,1,0:T(8,128)(2,1)}), bf16[32,32,256]{2,1,0:T(8,128)(2,1)S(1)}, u32[]{:S(2)}, u32[]{:S(2)}) async-start(bf16[32,32,256]{2,1,0:T(8,128)(2,1)} %get-tuple-element.24), calls=%async_computation | async-start | bytes 1048576 | tf_op jit(solution)/shard_map/all_to_all | solution.py:266
  14.3 0.0 copy-done.2
  14.4 3.3 %collective-permute-start.3 = (bf16[256,256]{1,0:T(8,128)(2,1)S(1)}, bf16[256,256]{1,0:T(8,128)(2,1)S(1)}, u32[]{:S(2)}, u32[]{:S(2)}) collective-permute-start(bf16[256,256]{1,0:T(8,128)(2,1)S(1)} %copy-done.2), channel_id=1, source_target_pairs={{32,64},{96,128},{160,192},{224,0},{64,32},{128,96},{192,160},{0,2... | collective-permute-start | bytes 393224 | tf_op jit(solution)/shard_map/ppermute | solution.py:235
  17.6 2.8 %collective-permute-start.2 = (bf16[256,256]{1,0:T(8,128)(2,1)S(1)}, bf16[256,256]{1,0:T(8,128)(2,1)S(1)}, u32[]{:S(2)}, u32[]{:S(2)}) collective-permute-start(bf16[256,256]{1,0:T(8,128)(2,1)S(1)} %copy-done.2), channel_id=1, source_target_pairs={{0,24},{8,0},{16,8},{24,16},{1,25},{9,1},{17,9},{25,17},{2,26},{10... | collective-permute-start | bytes 393224 | tf_op jit(solution)/shard_map/ppermute | solution.py:230
  20.4 0.8 collective-permute-start.1
  21.2 0.9 %collective-permute-start = (bf16[256,256]{1,0:T(8,128)(2,1)S(1)}, bf16[256,256]{1,0:T(8,128)(2,1)S(1)}, u32[]{:S(2)}, u32[]{:S(2)}) collective-permute-start(bf16[256,256]{1,0:T(8,128)(2,1)S(1)} %copy-done.2), channel_id=1, source_target_pairs={{0,8},{8,16},{16,24},{24,0},{1,9},{9,17},{17,25},{25,1},{2,10},{10... | collective-permute-start | bytes 393224 | tf_op jit(solution)/shard_map/ppermute | solution.py:230
  22.1 10.6 %collective-permute-done.3.refs_5_ = bf16[256,256]{1,0:T(8,128)(2,1)S(1)} collective-permute-done((bf16[256,256]{1,0:T(8,128)(2,1)S(1)}, bf16[256,256]{1,0:T(8,128)(2,1)S(1)}, u32[]{:S(2)}, u32[]{:S(2)}) %collective-permute-start.3) | collective-permute-done | bytes 131104 | tf_op jit(solution)/shard_map/ppermute | solution.py:235
  32.6 2.8 %collective-permute-start.6 = (bf16[256,256]{1,0:T(8,128)(2,1)S(1)}, bf16[256,256]{1,0:T(8,128)(2,1)S(1)}, u32[]{:S(2)}, u32[]{:S(2)}) collective-permute-start(bf16[256,256]{1,0:T(8,128)(2,1)S(1)} %collective-permute-done.3.refs_5_), channel_id=1, source_target_pairs={{0,24},{8,0},{16,8},{24,16},{1,25},{9,1},{17,9},{25,17},{2,26},{10... | collective-permute-start | bytes 393224 | tf_op jit(solution)/shard_map/ppermute | solution.py:230
  35.4 0.8 collective-permute-start.5
  36.2 0.0 collective-permute-done.2.refs_4_
  36.2 0.9 %collective-permute-start.4 = (bf16[256,256]{1,0:T(8,128)(2,1)S(1)}, bf16[256,256]{1,0:T(8,128)(2,1)S(1)}, u32[]{:S(2)}, u32[]{:S(2)}) collective-permute-start(bf16[256,256]{1,0:T(8,128)(2,1)S(1)} %collective-permute-done.3.refs_5_), channel_id=1, source_target_pairs={{0,8},{8,16},{16,24},{24,0},{1,9},{9,17},{17,25},{25,1},{2,10},{10... | collective-permute-start | bytes 393224 | tf_op jit(solution)/shard_map/ppermute | solution.py:230
  37.1 0.1 pad_add_fusion.where_ref
  37.2 0.0 collective-permute-done.1.refs_3_
  37.2 0.0 collective-permute-done.refs_2_
  37.2 3.6 %collective-permute-done.6.refs_8_ = bf16[256,256]{1,0:T(8,128)(2,1)S(1)} collective-permute-done((bf16[256,256]{1,0:T(8,128)(2,1)S(1)}, bf16[256,256]{1,0:T(8,128)(2,1)S(1)}, u32[]{:S(2)}, u32[]{:S(2)}) %collective-permute-start.6) | collective-permute-done | bytes 131104 | tf_op jit(solution)/shard_map/ppermute | solution.py:230
  40.7 2.3 %collective-permute-done.5.refs_7_ = bf16[256,256]{1,0:T(8,128)(2,1)S(1)} collective-permute-done((bf16[256,256]{1,0:T(8,128)(2,1)S(1)}, bf16[256,256]{1,0:T(8,128)(2,1)S(1)}, u32[]{:S(2)}, u32[]{:S(2)}) %collective-permute-start.5) | collective-permute-done | bytes 131104 | tf_op jit(solution)/shard_map/ppermute | solution.py:230
  43.0 1.4 %collective-permute-done.4.refs_6_ = bf16[256,256]{1,0:T(8,128)(2,1)S(1)} collective-permute-done((bf16[256,256]{1,0:T(8,128)(2,1)S(1)}, bf16[256,256]{1,0:T(8,128)(2,1)S(1)}, u32[]{:S(2)}, u32[]{:S(2)}) %collective-permute-start.4) | collective-permute-done | bytes 131104 | tf_op jit(solution)/shard_map/ppermute | solution.py:230
  44.4 0.0 all-to-all-done
  44.4 0.0 copy-done
  44.4 0.0 copy-done.1
  44.4 4.8 %forward.1 = (bf16[128,512]{1,0:T(8,128)(2,1)S(1)}, bf16[128,512]{1,0:T(8,128)(2,1)S(1)}, bf16[128,512]{1,0:T(8,128)(2,1)S(1)}, bf16[128,512]{1,0:T(8,128)(2,1)S...) custom-call(s32[4]{0:T(128)S(1)} %pad_add_fusion.where_ref, ...), custom_call_target="tpu_custom_call" | custom-call | flops 939524096 | bytes 2097152 | tf_op jit(solution)/shard_map/forward/pallas_call | solution.py:276
  49.2 4.8 %all-to-all-start.1 = ((f32[8,24,256]{2,1,0:T(8,128)}), f32[8,24,256]{2,1,0:T(8,128)S(1)}, u32[]{:S(2)}, u32[]{:S(2)}) async-start(f32[8,24,256]{2,1,0:T(8,128)} %get-tuple-element.27), calls=%async_computation.1 | async-start | bytes 393216 | tf_op jit(solution)/shard_map/all_to_all | solution.py:296
  54.0 1.5 %collective-permute-start.10 = (bf16[128,512]{1,0:T(8,128)(2,1)S(1)}, bf16[128,512]{1,0:T(8,128)(2,1)S(1)}, u32[]{:S(2)}, u32[]{:S(2)}) collective-permute-start(bf16[128,512]{1,0:T(8,128)(2,1)S(1)} %get-tuple-element.33), channel_id=1, source_target_pairs={{0,8},{8,16},{16,24},{24,0},{1,9},{9,17},{17,25},{25,1},{2,10},{10... | collective-permute-start | bytes 393224 | tf_op jit(solution)/shard_map/ppermute | solution.py:230
  55.4 2.7 %collective-permute-start.11 = (bf16[128,512]{1,0:T(8,128)(2,1)S(1)}, bf16[128,512]{1,0:T(8,128)(2,1)S(1)}, u32[]{:S(2)}, u32[]{:S(2)}) collective-permute-start(bf16[128,512]{1,0:T(8,128)(2,1)S(1)} %get-tuple-element.34), channel_id=1, source_target_pairs={{0,16},{8,24},{16,0},{24,8},{1,17},{9,25},{17,1},{25,9},{2,18},{10... | collective-permute-start | bytes 393224 | tf_op jit(solution)/shard_map/ppermute | solution.py:230
  58.1 1.5 %collective-permute-start.12 = (bf16[128,512]{1,0:T(8,128)(2,1)S(1)}, bf16[128,512]{1,0:T(8,128)(2,1)S(1)}, u32[]{:S(2)}, u32[]{:S(2)}) collective-permute-start(bf16[128,512]{1,0:T(8,128)(2,1)S(1)} %get-tuple-element.35), channel_id=1, source_target_pairs={{0,24},{8,0},{16,8},{24,16},{1,25},{9,1},{17,9},{25,17},{2,26},{10... | collective-permute-start | bytes 393224 | tf_op jit(solution)/shard_map/ppermute | solution.py:230
  59.6 0.2 all-to-all-done.1.refs_3_.got_ref
  59.7 5.2 %backward.1 = (bf16[128,512]{1,0:T(8,128)(2,1)S(1)}, bf16[128,512]{1,0:T(8,128)(2,1)S(1)}, bf16[128,512]{1,0:T(8,128)(2,1)S(1)}, bf16[128,512]{1,0:T(8,128)(2,1)...) custom-call(s32[4]{0:T(128)S(1)} %pad_add_fusion.where_ref, ...), custom_call_target="tpu_custom_call" | custom-call | flops 2348810240 | bytes 2097152 | tf_op jit(solution)/shard_map/backward/pallas_call | solution.py:298
  64.9 1.1 %collective-permute-start.7 = (bf16[128,512]{1,0:T(8,128)(2,1)S(1)}, bf16[128,512]{1,0:T(8,128)(2,1)S(1)}, u32[]{:S(2)}, u32[]{:S(2)}) collective-permute-start(bf16[128,512]{1,0:T(8,128)(2,1)S(1)} %get-tuple-element.29), channel_id=1, source_target_pairs={{0,8},{8,16},{16,24},{24,0},{1,9},{9,17},{17,25},{25,1},{2,10},{10... | collective-permute-start | bytes 393224 | tf_op jit(solution)/shard_map/ppermute | solution.py:230
  66.0 2.1 %collective-permute-start.8 = (bf16[128,512]{1,0:T(8,128)(2,1)S(1)}, bf16[128,512]{1,0:T(8,128)(2,1)S(1)}, u32[]{:S(2)}, u32[]{:S(2)}) collective-permute-start(bf16[128,512]{1,0:T(8,128)(2,1)S(1)} %get-tuple-element.30), channel_id=1, source_target_pairs={{0,16},{8,24},{16,0},{24,8},{1,17},{9,25},{17,1},{25,9},{2,18},{10... | collective-permute-start | bytes 393224 | tf_op jit(solution)/shard_map/ppermute | solution.py:230
  68.1 0.0 collective-permute-done.10.refs_1_
  68.1 0.7 collective-permute-start.9
  68.8 0.0 collective-permute-done.11.refs_2_
  68.8 1.9 %collective-permute-start.14 = (bf16[256,256]{1,0:T(8,128)(2,1)S(1)}, bf16[256,256]{1,0:T(8,128)(2,1)S(1)}, u32[]{:S(2)}, u32[]{:S(2)}) collective-permute-start(bf16[256,256]{1,0:T(8,128)(2,1)S(1)} %get-tuple-element.39), channel_id=1, source_target_pairs={{0,64},{192,0},{224,32},{1,65},{193,1},{225,33},{2,66},{194,2},{22... | collective-permute-start | bytes 393224 | tf_op jit(solution)/shard_map/ppermute | solution.py:317
  70.7 0.0 collective-permute-done.12.refs_3_
  70.7 3.7 %collective-permute-start.15 = (bf16[256,256]{1,0:T(8,128)(2,1)S(1)}, bf16[256,256]{1,0:T(8,128)(2,1)S(1)}, u32[]{:S(2)}, u32[]{:S(2)}) collective-permute-start(bf16[256,256]{1,0:T(8,128)(2,1)S(1)} %get-tuple-element.40), channel_id=1, source_target_pairs={{0,128},{128,0},{160,32},{192,64},{224,96},{1,129},{129,1},{161,33... | collective-permute-start | bytes 393224 | tf_op jit(solution)/shard_map/ppermute | solution.py:317
  74.5 0.7 mix.1
  75.2 0.0 collective-permute-done.7.refs_1_
  75.2 3.6 %collective-permute-start.16 = (bf16[256,256]{1,0:T(8,128)(2,1)S(1)}, bf16[256,256]{1,0:T(8,128)(2,1)S(1)}, u32[]{:S(2)}, u32[]{:S(2)}) collective-permute-start(bf16[256,256]{1,0:T(8,128)(2,1)S(1)} %get-tuple-element.41), channel_id=1, source_target_pairs={{0,192},{64,0},{96,32},{128,64},{160,96},{192,128},{224,160},{1,19... | collective-permute-start | bytes 393224 | tf_op jit(solution)/shard_map/ppermute | solution.py:317
  78.8 0.0 collective-permute-done.8.refs_2_
  78.8 0.0 collective-permute-done.9.refs_3_
  78.9 0.1 collective-permute-start.13
  79.0 0.1 collective-permute-done.14.refs_7_
  79.1 2.5 %collective-permute-done.15.refs_8_ = bf16[256,256]{1,0:T(8,128)(2,1)S(1)} collective-permute-done((bf16[256,256]{1,0:T(8,128)(2,1)S(1)}, bf16[256,256]{1,0:T(8,128)(2,1)S(1)}, u32[]{:S(2)}, u32[]{:S(2)}) %collective-permute-start.15) | collective-permute-done | bytes 131104 | tf_op jit(solution)/shard_map/ppermute | solution.py:317
  81.6 2.7 %collective-permute-done.16.refs_9_ = bf16[256,256]{1,0:T(8,128)(2,1)S(1)} collective-permute-done((bf16[256,256]{1,0:T(8,128)(2,1)S(1)}, bf16[256,256]{1,0:T(8,128)(2,1)S(1)}, u32[]{:S(2)}, u32[]{:S(2)}) %collective-permute-start.16) | collective-permute-done | bytes 131104 | tf_op jit(solution)/shard_map/ppermute | solution.py:317
  84.3 0.9 %collective-permute-done.13.refs_5_ = bf16[128,512]{1,0:T(8,128)(2,1)S(1)} collective-permute-done((bf16[128,512]{1,0:T(8,128)(2,1)S(1)}, bf16[128,512]{1,0:T(8,128)(2,1)S(1)}, u32[]{:S(2)}, u32[]{:S(2)}) %collective-permute-start.13) | collective-permute-done | bytes 131104 | tf_op jit(solution)/shard_map/ppermute | solution.py:235
  85.2 0.9 %final.1 = (bf16[256,128]{1,0:T(8,128)(2,1)}, f32[256,128]{1,0:T(8,128)}, f32[256,128]{1,0:T(8,128)}, f32[256,128]{1,0:T(8,128)}) custom-call(bf16[128,512]{1,0:T(8,128)(2,1)S(1)} %get-tuple-element.28.refs_0_, bf16[128,512]{1,0:T(8,128)(2,1)S(1)} %collective-permute-done.7.refs_1_, bf16[128,512]{1,0:T(8,128)(2,1)S(1)} %collective-permute-done.8.refs_2_, ...), custom_call_target="tpu_custom_call" | custom-call | tf_op jit(solution)/shard_map/final/pallas_call | solution.py:331
  (2 shorter events, 0.0 us)
Async XLA Ops:
  2.5 11.9 %copy-start.2 = (bf16[256,256]{1,0:T(8,128)(2,1)S(1)}, bf16[256,256]{1,0:T(8,128)(2,1)}, u32[]{:S(2)}) copy-start(bf16[256,256]{1,0:T(8,128)(2,1)} %get-tuple-element.23) | copy-start | bytes 393220
  2.5 41.9 %copy-start = (bf16[256,128]{1,0:T(8,128)(2,1)S(1)}, bf16[256,128]{1,0:T(8,128)(2,1)}, u32[]{:S(2)}) copy-start(bf16[256,128]{1,0:T(8,128)(2,1)} %refs_0_.1) | copy-start | bytes 196612
  2.5 41.9 %copy-start.1 = (bf16[256,128]{1,0:T(8,128)(2,1)S(1)}, bf16[256,128]{1,0:T(8,128)(2,1)}, u32[]{:S(2)}) copy-start(bf16[256,128]{1,0:T(8,128)(2,1)} %refs_1_.1) | copy-start | bytes 196612
  2.5 41.9 %all-to-all-start = ((bf16[32,32,256]{2,1,0:T(8,128)(2,1)}), bf16[32,32,256]{2,1,0:T(8,128)(2,1)S(1)}, u32[]{:S(2)}, u32[]{:S(2)}) async-start(bf16[32,32,256]{2,1,0:T(8,128)(2,1)} %get-tuple-element.24), calls=%async_computation | async-start | bytes 1048576 | tf_op jit(solution)/shard_map/all_to_all | solution.py:266
  14.4 18.3 %collective-permute-start.3 = (bf16[256,256]{1,0:T(8,128)(2,1)S(1)}, bf16[256,256]{1,0:T(8,128)(2,1)S(1)}, u32[]{:S(2)}, u32[]{:S(2)}) collective-permute-start(bf16[256,256]{1,0:T(8,128)(2,1)S(1)} %copy-done.2), channel_id=1, source_target_pairs={{32,64},{96,128},{160,192},{224,0},{64,32},{128,96},{192,160},{0,2... | collective-permute-start | bytes 393224 | tf_op jit(solution)/shard_map/ppermute | solution.py:235
  17.6 18.6 %collective-permute-start.2 = (bf16[256,256]{1,0:T(8,128)(2,1)S(1)}, bf16[256,256]{1,0:T(8,128)(2,1)S(1)}, u32[]{:S(2)}, u32[]{:S(2)}) collective-permute-start(bf16[256,256]{1,0:T(8,128)(2,1)S(1)} %copy-done.2), channel_id=1, source_target_pairs={{0,24},{8,0},{16,8},{24,16},{1,25},{9,1},{17,9},{25,17},{2,26},{10... | collective-permute-start | bytes 393224 | tf_op jit(solution)/shard_map/ppermute | solution.py:230
  20.4 16.8 %collective-permute-start.1 = (bf16[256,256]{1,0:T(8,128)(2,1)S(1)}, bf16[256,256]{1,0:T(8,128)(2,1)S(1)}, u32[]{:S(2)}, u32[]{:S(2)}) collective-permute-start(bf16[256,256]{1,0:T(8,128)(2,1)S(1)} %copy-done.2), channel_id=1, source_target_pairs={{0,16},{8,24},{16,0},{24,8},{1,17},{9,25},{17,1},{25,9},{2,18},{10... | collective-permute-start | bytes 393224 | tf_op jit(solution)/shard_map/ppermute | solution.py:230
  21.2 16.0 %collective-permute-start = (bf16[256,256]{1,0:T(8,128)(2,1)S(1)}, bf16[256,256]{1,0:T(8,128)(2,1)S(1)}, u32[]{:S(2)}, u32[]{:S(2)}) collective-permute-start(bf16[256,256]{1,0:T(8,128)(2,1)S(1)} %copy-done.2), channel_id=1, source_target_pairs={{0,8},{8,16},{16,24},{24,0},{1,9},{9,17},{17,25},{25,1},{2,10},{10... | collective-permute-start | bytes 393224 | tf_op jit(solution)/shard_map/ppermute | solution.py:230
  32.6 8.1 %collective-permute-start.6 = (bf16[256,256]{1,0:T(8,128)(2,1)S(1)}, bf16[256,256]{1,0:T(8,128)(2,1)S(1)}, u32[]{:S(2)}, u32[]{:S(2)}) collective-permute-start(bf16[256,256]{1,0:T(8,128)(2,1)S(1)} %collective-permute-done.3.refs_5_), channel_id=1, source_target_pairs={{0,24},{8,0},{16,8},{24,16},{1,25},{9,1},{17,9},{25,17},{2,26},{10... | collective-permute-start | bytes 393224 | tf_op jit(solution)/shard_map/ppermute | solution.py:230
  35.4 7.6 %collective-permute-start.5 = (bf16[256,256]{1,0:T(8,128)(2,1)S(1)}, bf16[256,256]{1,0:T(8,128)(2,1)S(1)}, u32[]{:S(2)}, u32[]{:S(2)}) collective-permute-start(bf16[256,256]{1,0:T(8,128)(2,1)S(1)} %collective-permute-done.3.refs_5_), channel_id=1, source_target_pairs={{0,16},{8,24},{16,0},{24,8},{1,17},{9,25},{17,1},{25,9},{2,18},{10... | collective-permute-start | bytes 393224 | tf_op jit(solution)/shard_map/ppermute | solution.py:230
  36.2 8.2 %collective-permute-start.4 = (bf16[256,256]{1,0:T(8,128)(2,1)S(1)}, bf16[256,256]{1,0:T(8,128)(2,1)S(1)}, u32[]{:S(2)}, u32[]{:S(2)}) collective-permute-start(bf16[256,256]{1,0:T(8,128)(2,1)S(1)} %collective-permute-done.3.refs_5_), channel_id=1, source_target_pairs={{0,8},{8,16},{16,24},{24,0},{1,9},{9,17},{17,25},{25,1},{2,10},{10... | collective-permute-start | bytes 393224 | tf_op jit(solution)/shard_map/ppermute | solution.py:230
  49.2 10.5 %all-to-all-start.1 = ((f32[8,24,256]{2,1,0:T(8,128)}), f32[8,24,256]{2,1,0:T(8,128)S(1)}, u32[]{:S(2)}, u32[]{:S(2)}) async-start(f32[8,24,256]{2,1,0:T(8,128)} %get-tuple-element.27), calls=%async_computation.1 | async-start | bytes 393216 | tf_op jit(solution)/shard_map/all_to_all | solution.py:296
  54.0 14.2 %collective-permute-start.10 = (bf16[128,512]{1,0:T(8,128)(2,1)S(1)}, bf16[128,512]{1,0:T(8,128)(2,1)S(1)}, u32[]{:S(2)}, u32[]{:S(2)}) collective-permute-start(bf16[128,512]{1,0:T(8,128)(2,1)S(1)} %get-tuple-element.33), channel_id=1, source_target_pairs={{0,8},{8,16},{16,24},{24,0},{1,9},{9,17},{17,25},{25,1},{2,10},{10... | collective-permute-start | bytes 393224 | tf_op jit(solution)/shard_map/ppermute | solution.py:230
  55.4 13.4 %collective-permute-start.11 = (bf16[128,512]{1,0:T(8,128)(2,1)S(1)}, bf16[128,512]{1,0:T(8,128)(2,1)S(1)}, u32[]{:S(2)}, u32[]{:S(2)}) collective-permute-start(bf16[128,512]{1,0:T(8,128)(2,1)S(1)} %get-tuple-element.34), channel_id=1, source_target_pairs={{0,16},{8,24},{16,0},{24,8},{1,17},{9,25},{17,1},{25,9},{2,18},{10... | collective-permute-start | bytes 393224 | tf_op jit(solution)/shard_map/ppermute | solution.py:230
  58.1 12.6 %collective-permute-start.12 = (bf16[128,512]{1,0:T(8,128)(2,1)S(1)}, bf16[128,512]{1,0:T(8,128)(2,1)S(1)}, u32[]{:S(2)}, u32[]{:S(2)}) collective-permute-start(bf16[128,512]{1,0:T(8,128)(2,1)S(1)} %get-tuple-element.35), channel_id=1, source_target_pairs={{0,24},{8,0},{16,8},{24,16},{1,25},{9,1},{17,9},{25,17},{2,26},{10... | collective-permute-start | bytes 393224 | tf_op jit(solution)/shard_map/ppermute | solution.py:230
  64.9 10.3 %collective-permute-start.7 = (bf16[128,512]{1,0:T(8,128)(2,1)S(1)}, bf16[128,512]{1,0:T(8,128)(2,1)S(1)}, u32[]{:S(2)}, u32[]{:S(2)}) collective-permute-start(bf16[128,512]{1,0:T(8,128)(2,1)S(1)} %get-tuple-element.29), channel_id=1, source_target_pairs={{0,8},{8,16},{16,24},{24,0},{1,9},{9,17},{17,25},{25,1},{2,10},{10... | collective-permute-start | bytes 393224 | tf_op jit(solution)/shard_map/ppermute | solution.py:230
  66.0 12.8 %collective-permute-start.8 = (bf16[128,512]{1,0:T(8,128)(2,1)S(1)}, bf16[128,512]{1,0:T(8,128)(2,1)S(1)}, u32[]{:S(2)}, u32[]{:S(2)}) collective-permute-start(bf16[128,512]{1,0:T(8,128)(2,1)S(1)} %get-tuple-element.30), channel_id=1, source_target_pairs={{0,16},{8,24},{16,0},{24,8},{1,17},{9,25},{17,1},{25,9},{2,18},{10... | collective-permute-start | bytes 393224 | tf_op jit(solution)/shard_map/ppermute | solution.py:230
  68.1 10.7 %collective-permute-start.9 = (bf16[128,512]{1,0:T(8,128)(2,1)S(1)}, bf16[128,512]{1,0:T(8,128)(2,1)S(1)}, u32[]{:S(2)}, u32[]{:S(2)}) collective-permute-start(bf16[128,512]{1,0:T(8,128)(2,1)S(1)} %get-tuple-element.31), channel_id=1, source_target_pairs={{0,24},{8,0},{16,8},{24,16},{1,25},{9,1},{17,9},{25,17},{2,26},{10... | collective-permute-start | bytes 393224 | tf_op jit(solution)/shard_map/ppermute | solution.py:230
  68.8 10.3 %collective-permute-start.14 = (bf16[256,256]{1,0:T(8,128)(2,1)S(1)}, bf16[256,256]{1,0:T(8,128)(2,1)S(1)}, u32[]{:S(2)}, u32[]{:S(2)}) collective-permute-start(bf16[256,256]{1,0:T(8,128)(2,1)S(1)} %get-tuple-element.39), channel_id=1, source_target_pairs={{0,64},{192,0},{224,32},{1,65},{193,1},{225,33},{2,66},{194,2},{22... | collective-permute-start | bytes 393224 | tf_op jit(solution)/shard_map/ppermute | solution.py:317
  70.7 10.9 %collective-permute-start.15 = (bf16[256,256]{1,0:T(8,128)(2,1)S(1)}, bf16[256,256]{1,0:T(8,128)(2,1)S(1)}, u32[]{:S(2)}, u32[]{:S(2)}) collective-permute-start(bf16[256,256]{1,0:T(8,128)(2,1)S(1)} %get-tuple-element.40), channel_id=1, source_target_pairs={{0,128},{128,0},{160,32},{192,64},{224,96},{1,129},{129,1},{161,33... | collective-permute-start | bytes 393224 | tf_op jit(solution)/shard_map/ppermute | solution.py:317
  75.2 9.1 %collective-permute-start.16 = (bf16[256,256]{1,0:T(8,128)(2,1)S(1)}, bf16[256,256]{1,0:T(8,128)(2,1)S(1)}, u32[]{:S(2)}, u32[]{:S(2)}) collective-permute-start(bf16[256,256]{1,0:T(8,128)(2,1)S(1)} %get-tuple-element.41), channel_id=1, source_target_pairs={{0,192},{64,0},{96,32},{128,64},{160,96},{192,128},{224,160},{1,19... | collective-permute-start | bytes 393224 | tf_op jit(solution)/shard_map/ppermute | solution.py:317
  78.9 6.3 %collective-permute-start.13 = (bf16[128,512]{1,0:T(8,128)(2,1)S(1)}, bf16[128,512]{1,0:T(8,128)(2,1)S(1)}, u32[]{:S(2)}, u32[]{:S(2)}) collective-permute-start(bf16[128,512]{1,0:T(8,128)(2,1)S(1)} %pad_maximum_fusion), channel_id=1, source_target_pairs={{32,64},{96,128},{160,192},{224,0},{64,32},{128,96},{192,160},{0,2... | collective-permute-start | bytes 393224 | tf_op jit(solution)/shard_map/ppermute | solution.py:235

commit v3 on v1

--- a/solution.py
+++ b/solution.py
@@ -9,8 +9,9 @@
 from jax.sharding import Mesh
 from jax.sharding import PartitionSpec as P
 
-Z = ("zj", "zp")
-SEQ = (*Z, "x")
+SEQ = ("z", "x")
+CLASSES = ((0, 1, 3, 6), (2, 4, 5, 7))
+NZ = 8
 VMEM = 24 << 20
 LOW = -1e30
 F32 = jnp.float32
@@ -63,8 +64,8 @@
         grad_ref[side, r * rows : (r + 1) * rows, :] = ref[:, width:]
 
 
-def each_unit(where_ref, last, unit):
-    own, full = where_ref[0], where_ref[0] + where_ref[1]
+def each_unit(own, other, last, unit):
+    full = own + other
 
     def whole(f, lane):
         side = jnp.where(f >= own, 1, 0)
@@ -87,6 +88,26 @@
 
 def folded(value, op):
     return op(value.reshape(value.shape[0] // 8, 8, value.shape[1]), axis=0)
+
+
+def paired(z):
+    return (z + 1 if z % 2 else z - 1) % NZ
+
+
+def class_of(z):
+    return next(members for members in CLASSES if z in members)
+
+
+def below(z, other):
+    return sum(k < other for k in class_of(z))
+
+
+def place(where_ref):
+    z, own, other = where_ref[0], jnp.int32(0), jnp.int32(0)
+    for at in range(NZ):
+        own = jnp.where(z == at, below(at, at), own)
+        other = jnp.where(z == at, below(at, paired(at)), other)
+    return own, other, where_ref[1], 1 - lax.rem(z, 2)
 
 
 def forward_kernel(rate, nx, where_ref, *refs):
@@ -94,7 +115,7 @@
     (own_q_ref, own_g_ref), q_refs, kv_ref, refs = refs[:2], refs[2 : n + 1], refs[n + 1], refs[n + 2 :]
     out_refs, (send_ref, query_ref, grad_ref), refs = refs[:nx], refs[nx : nx + 3], refs[nx + 3 :]
     s_ref, stat_ref, o_ref, m_ref, l_ref, sems = refs
-    x, even = where_ref[2], where_ref[3]
+    own, other, x, even = place(where_ref)
     rows, width = kv_ref.shape[1], kv_ref.shape[2] // 2
     moves = [
         pltpu.make_async_copy(own_q_ref, query_ref.at[0, :rows, :], sems.at[0]),
@@ -122,11 +143,11 @@
         o_ref[lane, side] += dot(kv_ref[j, :, width:], p.astype(BF16), TN)
 
     last = s_ref.shape[0] - 1
-    each_unit(where_ref, last, score)
+    each_unit(own, other, last, score)
     for side in range(2):
         both = jnp.maximum(m_ref[0, side], m_ref[1, side])
         m_ref[0, side, 0:1, :] = jnp.maximum(jnp.max(both, axis=0, keepdims=True), LOW / 2)
-    each_unit(where_ref, last, weigh)
+    each_unit(own, other, last, weigh)
     for side in range(2):
         total = jnp.sum(l_ref[0, side] + l_ref[1, side], axis=0, keepdims=True)
         o_ref[0, side] += o_ref[1, side]
@@ -149,7 +170,7 @@
     nj = kv_ref.shape[0]
     out_refs, key_refs, refs = refs[:nx], refs[nx : nx + nj], refs[nx + nj :]
     dq_ref, norm_ref, delta_ref, acc_ref, row_ref = refs
-    x, even = where_ref[2], where_ref[3]
+    own, other, x, even = place(where_ref)
     rows, width = kv_ref.shape[1], kv_ref.shape[2] // 2
     dq_ref[...] = jnp.zeros_like(dq_ref)
     acc_ref[...] = jnp.zeros_like(acc_ref)
@@ -178,9 +199,9 @@
         acc_ref[lane, j, :, :width] += dot(ds, query_ref[side], NN)
         dq_ref[lane, side] += dot(k, ds, TN)
 
-    each_unit(where_ref, 0, unit)
+    each_unit(own, other, 0, unit)
     for step in range(nj):
-        to = lax.rem(where_ref[0] + step, nj)
+        to = lax.rem(own + step, nj)
         both = acc_ref[0, to] + acc_ref[1, to]
         key_refs[step][:, :width] = (both[:, :width] * scaling).astype(BF16)
         key_refs[step][:, width:] = both[:, width:].astype(BF16)
@@ -194,7 +215,7 @@
 
 def mix_kernel(nx, where_ref, got_ref, *refs):
     part_refs, outs = refs[:nx], refs[nx:]
-    x, even = where_ref[2], where_ref[3]
+    _, _, x, even = place(where_ref)
     n = 2 * nx
     width, rows = part_refs[0].shape[0], part_refs[0].shape[1] // 2
     for side in range(2):
@@ -230,14 +251,22 @@
     return lax.ppermute(value, axis, [(i, (i + step) % count) for i in range(count)])
 
 
-def swapped(value, count):
-    pairs = [(i, (i + 1) % count) for i in range(1, count, 2)]
-    return lax.ppermute(value, Z, pairs + [(j, i) for i, j in pairs])
+def swapped(value):
+    return lax.ppermute(value, "z", [(z, paired(z)) for z in range(NZ)])
+
+
+def worked(step):
+    pairs = []
+    for z in range(NZ):
+        members = class_of(z)
+        to = members[(members.index(z) + step) % len(members)]
+        if to <= max(z, paired(z)):
+            pairs.append((z, to))
+    return pairs
 
 
 def per_device(nj, nx, nh, queries, keys, values, out_grad):
     rows, width = queries.shape
-    nz = 2 * nj
     scaling = 1.0 / math.sqrt(width)
     rate = scaling * math.log2(math.e)
     smem = pl.BlockSpec(memory_space=pltpu.SMEM)
@@ -254,15 +283,16 @@
         compiler_params=pltpu.CompilerParams(vmem_limit_bytes=60 << 20),
         name="prepare",
     )(queries, out_grad, keys, values)
-    other_own = swapped(own, nz)
+    other_own = swapped(own)
     blocks = [own, shifted(own, "x", nx, 1)]
     blocks += [shifted(own, "x", nx, r) for r in range(2, nx)]
     blocks += [other_own] + [shifted(other_own, "x", nx, r) for r in range(1, nx)]
-    kv = lax.all_to_all(mixed, ("zj", "head"), 0, 0, tiled=True)
+    peers = [[z * nh + h for z in members for h in range(nh)] for members in CLASSES]
+    kv = lax.all_to_all(
+        mixed, ("z", "head"), 0, 0, axis_index_groups=peers, tiled=True
+    )
     kv = kv.reshape(nj, rows, 2 * width)
-    zj, zp, x = (lax.axis_index(a) for a in SEQ)
-    other = jnp.where(zp == 0, jnp.where(zj == 0, nj, zj), lax.rem(zj + 1, nj))
-    where = jnp.stack([zj, other, x, 1 - zp]).astype(jnp.int32)
+    where = jnp.stack([lax.axis_index(a) for a in SEQ]).astype(jnp.int32)
     pairs = 7 * rows * nx * rows * width
     units = (2 * nj - 1, rows, nx * rows)
     stat = (6 * nx, rows)
@@ -287,7 +317,9 @@
         cost_estimate=pl.CostEstimate(flops=4 * pairs, bytes_accessed=2 << 20, transcendentals=0),
         name="forward",
     )(where, queries, out_grad, *blocks[1:], kv)
-    groups = [[z * nx + i for z in (m, (m + 1) % nz) for i in range(nx)] for m in range(1, nz, 2)]
+    groups = [
+        [z * nx + i for z in (m, paired(m)) for i in range(nx)] for m in range(1, NZ, 2)
+    ]
     got = lax.all_to_all(sent, SEQ, 0, 0, axis_index_groups=groups, tiled=True)
     offers = [offers[0]] + [shifted(offers[-r % nx], "x", nx, r) for r in range(1, nx)]
     both = pl.pallas_call(
@@ -309,7 +341,7 @@
     )(where, all_q, all_g, kv, got)
     parts, dkv = both[:nx], both[nx:]
     parts = [parts[0]] + [shifted(parts[-r % nx], "x", nx, r) for r in range(1, nx)]
-    dkv = [dkv[0]] + [shifted(dkv[r], "zj", nj, r) for r in range(1, nj)]
+    dkv = [dkv[0]] + [lax.ppermute(dkv[r], "z", worked(r)) for r in range(nj - 1, 0, -1)]
     near, far = pl.pallas_call(
         functools.partial(mix_kernel, nx),
         out_shape=(
@@ -321,8 +353,8 @@
         compiler_params=pltpu.CompilerParams(vmem_limit_bytes=8 << 20),
         name="mix",
     )(where, got, *offers)
-    back = functools.reduce(jnp.add, [p[:, rows:].astype(F32) for p in parts]).astype(BF16)
-    back = swapped(jnp.concatenate([back, far], axis=1), nz)
+    back = functools.reduce(jnp.add, [p[:, rows:].astype(F32) for p in parts])
+    back = swapped(jnp.concatenate([back.astype(BF16), far], axis=1))
     return pl.pallas_call(
         functools.partial(final_kernel, nx, nj),
         out_shape=(jax.ShapeDtypeStruct((rows, width), BF16),)
@@ -336,9 +368,9 @@
 
 def solution(mesh):
     nh = mesh.shape["head"]
-    split = Mesh(mesh.devices.reshape(4, 2, -1, nh), (*SEQ, "head"))
+    split = Mesh(mesh.devices.reshape(NZ, -1, nh), (*SEQ, "head"))
     return jax.shard_map(
-        functools.partial(per_device, 4, split.shape["x"], nh),
+        functools.partial(per_device, len(CLASSES[0]), split.shape["x"], nh),
         mesh=split,
         in_specs=(P(SEQ, "head"), P((*SEQ, "head"), None), P((*SEQ, "head"), None), P(SEQ, "head")),
         out_specs=(P(SEQ, "head"),) * 4,

time: 87.8 us -> 85.6 us (0.975)
  waiting for transfers between devices: 26.3 us -> 23.7 us
    ppermute x2 -> x5, starting transfers between devices: 3.62 us -> 12.6 us  [the longest x3 8.31 us: per_device(): lax.ppermute(dkv[r], 'z', worked(r))]
    ppermute x15 -> x12, starting transfers between devices: 25.7 us -> 18.3 us  [shifted(): lax.ppermute(value, axis, [(i, (i + step) % count) for i in range(count)])]
    ppermute x15 -> x12, waiting for transfers between devices: 14.3 us -> 7.75 us  [shifted(): lax.ppermute(value, axis, [(i, (i + step) % count) for i in range(count)])]
    ppermute x2 -> x5, waiting for transfers between devices: 11.8 us -> 15.8 us  [the longest x2 8.87 us: swapped(): return lax.ppermute(value, 'z', [(z, paired(z)) for z in range(NZ)])]
    all_to_all x1, starting transfers between devices: 11.8 us -> 11 us  [per_device(): lax.all_to_all(mixed, ('z', 'head'), 0, 0, axis_index_groups=peers, tiled...]
  transfers between devices with their start and end apart: 19 -> 19, of which waited for: 9 -> 8; matrix products, arithmetic and copies ran while one was open for 0% -> 0% of each run, Pallas kernels for 7% -> 7%
where the time goes in v3:
time: 85.6 us; the launch traced here: 84.6 us
  starting transfers between devices  46.5 us (54%)
  waiting for transfers between devices  23.7 us (28%)
  Pallas kernels  13.4 us (16%)
    ppermute x12, starting transfers between devices, shifted(): lax.ppermute(value, axis, [(i, (i + step) % count) for i in range(count)])  18.3 us
    all_to_all x1, starting transfers between devices, per_device(): lax.all_to_all(mixed, ('z', 'head'), 0, 0, axis_index_groups=peers, tiled...  11 us
    ppermute x2, waiting for transfers between devices, swapped(): return lax.ppermute(value, 'z', [(z, paired(z)) for z in range(NZ)])  8.87 us
    ppermute x3, starting transfers between devices, per_device(): lax.ppermute(dkv[r], 'z', worked(r))  8.31 us
    ppermute x12, waiting for transfers between devices, shifted(): lax.ppermute(value, axis, [(i, (i + step) % count) for i in range(count)])  7.75 us
    ppermute x3, waiting for transfers between devices, per_device(): lax.ppermute(dkv[r], 'z', worked(r))  6.95 us
    pallas_call x1, Pallas kernels, per_device(): pl.pallas_call(functools.partial(backward_kernel, rate, scaling, nx), out...  5.16 us
    pallas_call x1, Pallas kernels, per_device(): pl.pallas_call(functools.partial(forward_kernel, rate, nx), out_shape=(ja...  4.77 us
  transfers between devices with their start and end apart: 19, of which 8 were waited for; matrix products, arithmetic and copies ran while one was open for 0% of the time, Pallas kernels for 7%

profile of v3, /device:TPU:8, one launch (start us, length us, event | category | flops | bytes accessed | tf_op | source)
XLA Modules:
  0.0 84.6 jit_solution(1363631871870055383)
XLA Ops:
  0.6 1.8 %prepare.1 = (bf16[256,256]{1,0:T(8,128)(2,1)}, bf16[32,32,256]{2,1,0:T(8,128)(2,1)}) custom-call(bf16[256,128]{1,0:T(8,128)(2,1)} %refs_0_.1, bf16[256,128]{1,0:T(8,128)(2,1)} %refs_1_.1, bf16[32,1024]{1,0:T(8,128)(2,1)} %k_ref.1, bf16[32,1024]{1,0:T(8,128)(2,1)} %v_ref.1), custom_call_target="tpu_custom_call" | custom-call | tf_op jit(solution)/shard_map/prepare/pallas_call | solution.py:274
  2.5 0.0 copy-start.2
  2.5 0.0 copy-start
  2.5 0.0 copy-start.1
  2.5 11.0 %all-to-all-start = ((bf16[32,32,256]{2,1,0:T(8,128)(2,1)}), bf16[32,32,256]{2,1,0:T(8,128)(2,1)S(1)}, u32[]{:S(2)}, u32[]{:S(2)}) async-start(bf16[32,32,256]{2,1,0:T(8,128)(2,1)} %get-tuple-element.24), calls=%async_computation | async-start | bytes 1048576 | tf_op jit(solution)/shard_map/all_to_all | solution.py:291
  13.5 0.0 copy-done.2
  13.5 4.2 %collective-permute-start.3 = (bf16[256,256]{1,0:T(8,128)(2,1)S(1)}, bf16[256,256]{1,0:T(8,128)(2,1)S(1)}, u32[]{:S(2)}, u32[]{:S(2)}) collective-permute-start(bf16[256,256]{1,0:T(8,128)(2,1)S(1)} %copy-done.2), channel_id=1, source_target_pairs={{0,224},{32,64},{64,32},{96,128},{128,96},{160,192},{192,160},{224... | collective-permute-start | bytes 393224 | tf_op jit(solution)/shard_map/ppermute | solution.py:255
  17.6 2.8 %collective-permute-start.2 = (bf16[256,256]{1,0:T(8,128)(2,1)S(1)}, bf16[256,256]{1,0:T(8,128)(2,1)S(1)}, u32[]{:S(2)}, u32[]{:S(2)}) collective-permute-start(bf16[256,256]{1,0:T(8,128)(2,1)S(1)} %copy-done.2), channel_id=1, source_target_pairs={{0,24},{8,0},{16,8},{24,16},{1,25},{9,1},{17,9},{25,17},{2,26},{10... | collective-permute-start | bytes 393224 | tf_op jit(solution)/shard_map/ppermute | solution.py:251
  20.4 0.8 collective-permute-start.1
  21.2 0.9 %collective-permute-start = (bf16[256,256]{1,0:T(8,128)(2,1)S(1)}, bf16[256,256]{1,0:T(8,128)(2,1)S(1)}, u32[]{:S(2)}, u32[]{:S(2)}) collective-permute-start(bf16[256,256]{1,0:T(8,128)(2,1)S(1)} %copy-done.2), channel_id=1, source_target_pairs={{0,8},{8,16},{16,24},{24,0},{1,9},{9,17},{17,25},{25,1},{2,10},{10... | collective-permute-start | bytes 393224 | tf_op jit(solution)/shard_map/ppermute | solution.py:251
  22.1 7.3 %collective-permute-done.3.refs_5_ = bf16[256,256]{1,0:T(8,128)(2,1)S(1)} collective-permute-done((bf16[256,256]{1,0:T(8,128)(2,1)S(1)}, bf16[256,256]{1,0:T(8,128)(2,1)S(1)}, u32[]{:S(2)}, u32[]{:S(2)}) %collective-permute-start.3) | collective-permute-done | bytes 131104 | tf_op jit(solution)/shard_map/ppermute | solution.py:255
  29.4 2.8 %collective-permute-start.6 = (bf16[256,256]{1,0:T(8,128)(2,1)S(1)}, bf16[256,256]{1,0:T(8,128)(2,1)S(1)}, u32[]{:S(2)}, u32[]{:S(2)}) collective-permute-start(bf16[256,256]{1,0:T(8,128)(2,1)S(1)} %collective-permute-done.3.refs_5_), channel_id=1, source_target_pairs={{0,24},{8,0},{16,8},{24,16},{1,25},{9,1},{17,9},{25,17},{2,26},{10... | collective-permute-start | bytes 393224 | tf_op jit(solution)/shard_map/ppermute | solution.py:251
  32.2 0.8 collective-permute-start.5
  33.0 0.0 collective-permute-done.2.refs_4_
  33.0 0.9 %collective-permute-start.4 = (bf16[256,256]{1,0:T(8,128)(2,1)S(1)}, bf16[256,256]{1,0:T(8,128)(2,1)S(1)}, u32[]{:S(2)}, u32[]{:S(2)}) collective-permute-start(bf16[256,256]{1,0:T(8,128)(2,1)S(1)} %collective-permute-done.3.refs_5_), channel_id=1, source_target_pairs={{0,8},{8,16},{16,24},{24,0},{1,9},{9,17},{17,25},{25,1},{2,10},{10... | collective-permute-start | bytes 393224 | tf_op jit(solution)/shard_map/ppermute | solution.py:251
  33.8 0.1 pad_add_fusion.where_ref
  33.9 0.0 collective-permute-done.1.refs_3_
  33.9 0.0 collective-permute-done.refs_2_
  33.9 4.1 %collective-permute-done.6.refs_8_ = bf16[256,256]{1,0:T(8,128)(2,1)S(1)} collective-permute-done((bf16[256,256]{1,0:T(8,128)(2,1)S(1)}, bf16[256,256]{1,0:T(8,128)(2,1)S(1)}, u32[]{:S(2)}, u32[]{:S(2)}) %collective-permute-start.6) | collective-permute-done | bytes 131104 | tf_op jit(solution)/shard_map/ppermute | solution.py:251
  38.0 2.0 %collective-permute-done.5.refs_7_ = bf16[256,256]{1,0:T(8,128)(2,1)S(1)} collective-permute-done((bf16[256,256]{1,0:T(8,128)(2,1)S(1)}, bf16[256,256]{1,0:T(8,128)(2,1)S(1)}, u32[]{:S(2)}, u32[]{:S(2)}) %collective-permute-start.5) | collective-permute-done | bytes 131104 | tf_op jit(solution)/shard_map/ppermute | solution.py:251
  40.0 1.6 %collective-permute-done.4.refs_6_ = bf16[256,256]{1,0:T(8,128)(2,1)S(1)} collective-permute-done((bf16[256,256]{1,0:T(8,128)(2,1)S(1)}, bf16[256,256]{1,0:T(8,128)(2,1)S(1)}, u32[]{:S(2)}, u32[]{:S(2)}) %collective-permute-start.4) | collective-permute-done | bytes 131104 | tf_op jit(solution)/shard_map/ppermute | solution.py:251
  41.6 0.0 all-to-all-done
  41.7 0.0 copy-done
  41.7 0.0 copy-done.1
  41.7 4.8 %forward.1 = (bf16[128,512]{1,0:T(8,128)(2,1)S(1)}, bf16[128,512]{1,0:T(8,128)(2,1)S(1)}, bf16[128,512]{1,0:T(8,128)(2,1)S(1)}, bf16[128,512]{1,0:T(8,128)(2,1)S...) custom-call(s32[2]{0:T(128)S(1)} %pad_add_fusion.where_ref, ...), custom_call_target="tpu_custom_call" | custom-call | flops 939524096 | bytes 2097152 | tf_op jit(solution)/shard_map/forward/pallas_call | solution.py:301
  46.4 4.8 %all-to-all-start.1 = ((f32[8,24,256]{2,1,0:T(8,128)}), f32[8,24,256]{2,1,0:T(8,128)S(1)}, u32[]{:S(2)}, u32[]{:S(2)}) async-start(f32[8,24,256]{2,1,0:T(8,128)} %get-tuple-element.27), calls=%async_computation.1 | async-start | bytes 393216 | tf_op jit(solution)/shard_map/all_to_all | solution.py:323
  51.2 1.5 %collective-permute-start.10 = (bf16[128,512]{1,0:T(8,128)(2,1)S(1)}, bf16[128,512]{1,0:T(8,128)(2,1)S(1)}, u32[]{:S(2)}, u32[]{:S(2)}) collective-permute-start(bf16[128,512]{1,0:T(8,128)(2,1)S(1)} %get-tuple-element.33), channel_id=1, source_target_pairs={{0,8},{8,16},{16,24},{24,0},{1,9},{9,17},{17,25},{25,1},{2,10},{10... | collective-permute-start | bytes 393224 | tf_op jit(solution)/shard_map/ppermute | solution.py:251
  52.7 2.7 %collective-permute-start.11 = (bf16[128,512]{1,0:T(8,128)(2,1)S(1)}, bf16[128,512]{1,0:T(8,128)(2,1)S(1)}, u32[]{:S(2)}, u32[]{:S(2)}) collective-permute-start(bf16[128,512]{1,0:T(8,128)(2,1)S(1)} %get-tuple-element.34), channel_id=1, source_target_pairs={{0,16},{8,24},{16,0},{24,8},{1,17},{9,25},{17,1},{25,9},{2,18},{10... | collective-permute-start | bytes 393224 | tf_op jit(solution)/shard_map/ppermute | solution.py:251
  55.3 1.5 %collective-permute-start.12 = (bf16[128,512]{1,0:T(8,128)(2,1)S(1)}, bf16[128,512]{1,0:T(8,128)(2,1)S(1)}, u32[]{:S(2)}, u32[]{:S(2)}) collective-permute-start(bf16[128,512]{1,0:T(8,128)(2,1)S(1)} %get-tuple-element.35), channel_id=1, source_target_pairs={{0,24},{8,0},{16,8},{24,16},{1,25},{9,1},{17,9},{25,17},{2,26},{10... | collective-permute-start | bytes 393224 | tf_op jit(solution)/shard_map/ppermute | solution.py:251
  56.8 0.2 all-to-all-done.1.refs_3_.got_ref
  57.0 5.2 %backward.1 = (bf16[128,512]{1,0:T(8,128)(2,1)S(1)}, bf16[128,512]{1,0:T(8,128)(2,1)S(1)}, bf16[128,512]{1,0:T(8,128)(2,1)S(1)}, bf16[128,512]{1,0:T(8,128)(2,1)...) custom-call(s32[2]{0:T(128)S(1)} %pad_add_fusion.where_ref, ...), custom_call_target="tpu_custom_call" | custom-call | flops 2348810240 | bytes 2097152 | tf_op jit(solution)/shard_map/backward/pallas_call | solution.py:325
  62.1 1.0 %collective-permute-start.7 = (bf16[128,512]{1,0:T(8,128)(2,1)S(1)}, bf16[128,512]{1,0:T(8,128)(2,1)S(1)}, u32[]{:S(2)}, u32[]{:S(2)}) collective-permute-start(bf16[128,512]{1,0:T(8,128)(2,1)S(1)} %get-tuple-element.29), channel_id=1, source_target_pairs={{0,8},{8,16},{16,24},{24,0},{1,9},{9,17},{17,25},{25,1},{2,10},{10... | collective-permute-start | bytes 393224 | tf_op jit(solution)/shard_map/ppermute | solution.py:251
  63.1 2.2 %collective-permute-start.8 = (bf16[128,512]{1,0:T(8,128)(2,1)S(1)}, bf16[128,512]{1,0:T(8,128)(2,1)S(1)}, u32[]{:S(2)}, u32[]{:S(2)}) collective-permute-start(bf16[128,512]{1,0:T(8,128)(2,1)S(1)} %get-tuple-element.30), channel_id=1, source_target_pairs={{0,16},{8,24},{16,0},{24,8},{1,17},{9,25},{17,1},{25,9},{2,18},{10... | collective-permute-start | bytes 393224 | tf_op jit(solution)/shard_map/ppermute | solution.py:251
  65.3 0.0 collective-permute-done.10.refs_1_
  65.3 0.6 collective-permute-start.9
  65.9 0.0 collective-permute-done.11.refs_2_
  65.9 4.5 %collective-permute-start.14 = (bf16[256,256]{1,0:T(8,128)(2,1)S(1)}, bf16[256,256]{1,0:T(8,128)(2,1)S(1)}, u32[]{:S(2)}, u32[]{:S(2)}) collective-permute-start(bf16[256,256]{1,0:T(8,128)(2,1)S(1)} %get-tuple-element.39), channel_id=1, source_target_pairs={{0,192},{32,0},{96,32},{128,64},{160,128},{192,96},{224,160},{1,19... | collective-permute-start | bytes 393224 | tf_op jit(solution)/shard_map/ppermute | solution.py:344
  70.4 0.0 collective-permute-done.12.refs_3_
  70.4 1.9 %collective-permute-start.15 = (bf16[256,256]{1,0:T(8,128)(2,1)S(1)}, bf16[256,256]{1,0:T(8,128)(2,1)S(1)}, u32[]{:S(2)}, u32[]{:S(2)}) collective-permute-start(bf16[256,256]{1,0:T(8,128)(2,1)S(1)} %get-tuple-element.40), channel_id=1, source_target_pairs={{0,96},{96,0},{160,64},{192,32},{224,128},{1,97},{97,1},{161,65},{... | collective-permute-start | bytes 393224 | tf_op jit(solution)/shard_map/ppermute | solution.py:344
  72.3 0.7 mix.1
  73.0 0.0 collective-permute-done.7.refs_1_
  73.0 1.9 %collective-permute-start.16 = (bf16[256,256]{1,0:T(8,128)(2,1)S(1)}, bf16[256,256]{1,0:T(8,128)(2,1)S(1)}, u32[]{:S(2)}, u32[]{:S(2)}) collective-permute-start(bf16[256,256]{1,0:T(8,128)(2,1)S(1)} %get-tuple-element.41), channel_id=1, source_target_pairs={{0,32},{192,0},{224,64},{1,33},{193,1},{225,65},{2,34},{194,2},{22... | collective-permute-start | bytes 393224 | tf_op jit(solution)/shard_map/ppermute | solution.py:344
  75.0 0.0 collective-permute-done.8.refs_2_
  75.0 0.0 collective-permute-done.9.refs_3_
  75.1 0.1 collective-permute-start.13
  75.2 0.0 collective-permute-done.14.refs_7_
  75.2 4.1 %collective-permute-done.15.refs_8_ = bf16[256,256]{1,0:T(8,128)(2,1)S(1)} collective-permute-done((bf16[256,256]{1,0:T(8,128)(2,1)S(1)}, bf16[256,256]{1,0:T(8,128)(2,1)S(1)}, u32[]{:S(2)}, u32[]{:S(2)}) %collective-permute-start.15) | collective-permute-done | bytes 131104 | tf_op jit(solution)/shard_map/ppermute | solution.py:344
  79.3 2.8 %collective-permute-done.16.refs_9_ = bf16[256,256]{1,0:T(8,128)(2,1)S(1)} collective-permute-done((bf16[256,256]{1,0:T(8,128)(2,1)S(1)}, bf16[256,256]{1,0:T(8,128)(2,1)S(1)}, u32[]{:S(2)}, u32[]{:S(2)}) %collective-permute-start.16) | collective-permute-done | bytes 131104 | tf_op jit(solution)/shard_map/ppermute | solution.py:344
  82.1 1.6 %collective-permute-done.13.refs_5_ = bf16[128,512]{1,0:T(8,128)(2,1)S(1)} collective-permute-done((bf16[128,512]{1,0:T(8,128)(2,1)S(1)}, bf16[128,512]{1,0:T(8,128)(2,1)S(1)}, u32[]{:S(2)}, u32[]{:S(2)}) %collective-permute-start.13) | collective-permute-done | bytes 131104 | tf_op jit(solution)/shard_map/ppermute | solution.py:255
  83.7 0.9 %final.1 = (bf16[256,128]{1,0:T(8,128)(2,1)}, f32[256,128]{1,0:T(8,128)}, f32[256,128]{1,0:T(8,128)}, f32[256,128]{1,0:T(8,128)}) custom-call(bf16[128,512]{1,0:T(8,128)(2,1)S(1)} %get-tuple-element.28.refs_0_, bf16[128,512]{1,0:T(8,128)(2,1)S(1)} %collective-permute-done.7.refs_1_, bf16[128,512]{1,0:T(8,128)(2,1)S(1)} %collective-permute-done.8.refs_2_, ...), custom_call_target="tpu_custom_call" | custom-call | tf_op jit(solution)/shard_map/final/pallas_call | solution.py:358
  (2 shorter events, 0.0 us)
Async XLA Ops:
  2.5 11.0 %copy-start.2 = (bf16[256,256]{1,0:T(8,128)(2,1)S(1)}, bf16[256,256]{1,0:T(8,128)(2,1)}, u32[]{:S(2)}) copy-start(bf16[256,256]{1,0:T(8,128)(2,1)} %get-tuple-element.23) | copy-start | bytes 393220
  2.5 39.2 %copy-start = (bf16[256,128]{1,0:T(8,128)(2,1)S(1)}, bf16[256,128]{1,0:T(8,128)(2,1)}, u32[]{:S(2)}) copy-start(bf16[256,128]{1,0:T(8,128)(2,1)} %refs_0_.1) | copy-start | bytes 196612
  2.5 39.2 %copy-start.1 = (bf16[256,128]{1,0:T(8,128)(2,1)S(1)}, bf16[256,128]{1,0:T(8,128)(2,1)}, u32[]{:S(2)}) copy-start(bf16[256,128]{1,0:T(8,128)(2,1)} %refs_1_.1) | copy-start | bytes 196612
  2.5 39.2 %all-to-all-start = ((bf16[32,32,256]{2,1,0:T(8,128)(2,1)}), bf16[32,32,256]{2,1,0:T(8,128)(2,1)S(1)}, u32[]{:S(2)}, u32[]{:S(2)}) async-start(bf16[32,32,256]{2,1,0:T(8,128)(2,1)} %get-tuple-element.24), calls=%async_computation | async-start | bytes 1048576 | tf_op jit(solution)/shard_map/all_to_all | solution.py:291
  13.5 15.9 %collective-permute-start.3 = (bf16[256,256]{1,0:T(8,128)(2,1)S(1)}, bf16[256,256]{1,0:T(8,128)(2,1)S(1)}, u32[]{:S(2)}, u32[]{:S(2)}) collective-permute-start(bf16[256,256]{1,0:T(8,128)(2,1)S(1)} %copy-done.2), channel_id=1, source_target_pairs={{0,224},{32,64},{64,32},{96,128},{128,96},{160,192},{192,160},{224... | collective-permute-start | bytes 393224 | tf_op jit(solution)/shard_map/ppermute | solution.py:255
  17.6 15.3 %collective-permute-start.2 = (bf16[256,256]{1,0:T(8,128)(2,1)S(1)}, bf16[256,256]{1,0:T(8,128)(2,1)S(1)}, u32[]{:S(2)}, u32[]{:S(2)}) collective-permute-start(bf16[256,256]{1,0:T(8,128)(2,1)S(1)} %copy-done.2), channel_id=1, source_target_pairs={{0,24},{8,0},{16,8},{24,16},{1,25},{9,1},{17,9},{25,17},{2,26},{10... | collective-permute-start | bytes 393224 | tf_op jit(solution)/shard_map/ppermute | solution.py:251
  20.4 13.5 %collective-permute-start.1 = (bf16[256,256]{1,0:T(8,128)(2,1)S(1)}, bf16[256,256]{1,0:T(8,128)(2,1)S(1)}, u32[]{:S(2)}, u32[]{:S(2)}) collective-permute-start(bf16[256,256]{1,0:T(8,128)(2,1)S(1)} %copy-done.2), channel_id=1, source_target_pairs={{0,16},{8,24},{16,0},{24,8},{1,17},{9,25},{17,1},{25,9},{2,18},{10... | collective-permute-start | bytes 393224 | tf_op jit(solution)/shard_map/ppermute | solution.py:251
  21.2 12.7 %collective-permute-start = (bf16[256,256]{1,0:T(8,128)(2,1)S(1)}, bf16[256,256]{1,0:T(8,128)(2,1)S(1)}, u32[]{:S(2)}, u32[]{:S(2)}) collective-permute-start(bf16[256,256]{1,0:T(8,128)(2,1)S(1)} %copy-done.2), channel_id=1, source_target_pairs={{0,8},{8,16},{16,24},{24,0},{1,9},{9,17},{17,25},{25,1},{2,10},{10... | collective-permute-start | bytes 393224 | tf_op jit(solution)/shard_map/ppermute | solution.py:251
  29.4 8.6 %collective-permute-start.6 = (bf16[256,256]{1,0:T(8,128)(2,1)S(1)}, bf16[256,256]{1,0:T(8,128)(2,1)S(1)}, u32[]{:S(2)}, u32[]{:S(2)}) collective-permute-start(bf16[256,256]{1,0:T(8,128)(2,1)S(1)} %collective-permute-done.3.refs_5_), channel_id=1, source_target_pairs={{0,24},{8,0},{16,8},{24,16},{1,25},{9,1},{17,9},{25,17},{2,26},{10... | collective-permute-start | bytes 393224 | tf_op jit(solution)/shard_map/ppermute | solution.py:251
  32.2 7.9 %collective-permute-start.5 = (bf16[256,256]{1,0:T(8,128)(2,1)S(1)}, bf16[256,256]{1,0:T(8,128)(2,1)S(1)}, u32[]{:S(2)}, u32[]{:S(2)}) collective-permute-start(bf16[256,256]{1,0:T(8,128)(2,1)S(1)} %collective-permute-done.3.refs_5_), channel_id=1, source_target_pairs={{0,16},{8,24},{16,0},{24,8},{1,17},{9,25},{17,1},{25,9},{2,18},{10... | collective-permute-start | bytes 393224 | tf_op jit(solution)/shard_map/ppermute | solution.py:251
  33.0 8.7 %collective-permute-start.4 = (bf16[256,256]{1,0:T(8,128)(2,1)S(1)}, bf16[256,256]{1,0:T(8,128)(2,1)S(1)}, u32[]{:S(2)}, u32[]{:S(2)}) collective-permute-start(bf16[256,256]{1,0:T(8,128)(2,1)S(1)} %collective-permute-done.3.refs_5_), channel_id=1, source_target_pairs={{0,8},{8,16},{16,24},{24,0},{1,9},{9,17},{17,25},{25,1},{2,10},{10... | collective-permute-start | bytes 393224 | tf_op jit(solution)/shard_map/ppermute | solution.py:251
  46.4 10.5 %all-to-all-start.1 = ((f32[8,24,256]{2,1,0:T(8,128)}), f32[8,24,256]{2,1,0:T(8,128)S(1)}, u32[]{:S(2)}, u32[]{:S(2)}) async-start(f32[8,24,256]{2,1,0:T(8,128)} %get-tuple-element.27), calls=%async_computation.1 | async-start | bytes 393216 | tf_op jit(solution)/shard_map/all_to_all | solution.py:323
  51.2 14.1 %collective-permute-start.10 = (bf16[128,512]{1,0:T(8,128)(2,1)S(1)}, bf16[128,512]{1,0:T(8,128)(2,1)S(1)}, u32[]{:S(2)}, u32[]{:S(2)}) collective-permute-start(bf16[128,512]{1,0:T(8,128)(2,1)S(1)} %get-tuple-element.33), channel_id=1, source_target_pairs={{0,8},{8,16},{16,24},{24,0},{1,9},{9,17},{17,25},{25,1},{2,10},{10... | collective-permute-start | bytes 393224 | tf_op jit(solution)/shard_map/ppermute | solution.py:251
  52.7 13.2 %collective-permute-start.11 = (bf16[128,512]{1,0:T(8,128)(2,1)S(1)}, bf16[128,512]{1,0:T(8,128)(2,1)S(1)}, u32[]{:S(2)}, u32[]{:S(2)}) collective-permute-start(bf16[128,512]{1,0:T(8,128)(2,1)S(1)} %get-tuple-element.34), channel_id=1, source_target_pairs={{0,16},{8,24},{16,0},{24,8},{1,17},{9,25},{17,1},{25,9},{2,18},{10... | collective-permute-start | bytes 393224 | tf_op jit(solution)/shard_map/ppermute | solution.py:251
  55.3 15.1 %collective-permute-start.12 = (bf16[128,512]{1,0:T(8,128)(2,1)S(1)}, bf16[128,512]{1,0:T(8,128)(2,1)S(1)}, u32[]{:S(2)}, u32[]{:S(2)}) collective-permute-start(bf16[128,512]{1,0:T(8,128)(2,1)S(1)} %get-tuple-element.35), channel_id=1, source_target_pairs={{0,24},{8,0},{16,8},{24,16},{1,25},{9,1},{17,9},{25,17},{2,26},{10... | collective-permute-start | bytes 393224 | tf_op jit(solution)/shard_map/ppermute | solution.py:251
  62.1 10.9 %collective-permute-start.7 = (bf16[128,512]{1,0:T(8,128)(2,1)S(1)}, bf16[128,512]{1,0:T(8,128)(2,1)S(1)}, u32[]{:S(2)}, u32[]{:S(2)}) collective-permute-start(bf16[128,512]{1,0:T(8,128)(2,1)S(1)} %get-tuple-element.29), channel_id=1, source_target_pairs={{0,8},{8,16},{16,24},{24,0},{1,9},{9,17},{17,25},{25,1},{2,10},{10... | collective-permute-start | bytes 393224 | tf_op jit(solution)/shard_map/ppermute | solution.py:251
  63.1 11.8 %collective-permute-start.8 = (bf16[128,512]{1,0:T(8,128)(2,1)S(1)}, bf16[128,512]{1,0:T(8,128)(2,1)S(1)}, u32[]{:S(2)}, u32[]{:S(2)}) collective-permute-start(bf16[128,512]{1,0:T(8,128)(2,1)S(1)} %get-tuple-element.30), channel_id=1, source_target_pairs={{0,16},{8,24},{16,0},{24,8},{1,17},{9,25},{17,1},{25,9},{2,18},{10... | collective-permute-start | bytes 393224 | tf_op jit(solution)/shard_map/ppermute | solution.py:251
  65.3 9.7 %collective-permute-start.9 = (bf16[128,512]{1,0:T(8,128)(2,1)S(1)}, bf16[128,512]{1,0:T(8,128)(2,1)S(1)}, u32[]{:S(2)}, u32[]{:S(2)}) collective-permute-start(bf16[128,512]{1,0:T(8,128)(2,1)S(1)} %get-tuple-element.31), channel_id=1, source_target_pairs={{0,24},{8,0},{16,8},{24,16},{1,25},{9,1},{17,9},{25,17},{2,26},{10... | collective-permute-start | bytes 393224 | tf_op jit(solution)/shard_map/ppermute | solution.py:251
  65.9 9.3 %collective-permute-start.14 = (bf16[256,256]{1,0:T(8,128)(2,1)S(1)}, bf16[256,256]{1,0:T(8,128)(2,1)S(1)}, u32[]{:S(2)}, u32[]{:S(2)}) collective-permute-start(bf16[256,256]{1,0:T(8,128)(2,1)S(1)} %get-tuple-element.39), channel_id=1, source_target_pairs={{0,192},{32,0},{96,32},{128,64},{160,128},{192,96},{224,160},{1,19... | collective-permute-start | bytes 393224 | tf_op jit(solution)/shard_map/ppermute | solution.py:344
  70.4 8.9 %collective-permute-start.15 = (bf16[256,256]{1,0:T(8,128)(2,1)S(1)}, bf16[256,256]{1,0:T(8,128)(2,1)S(1)}, u32[]{:S(2)}, u32[]{:S(2)}) collective-permute-start(bf16[256,256]{1,0:T(8,128)(2,1)S(1)} %get-tuple-element.40), channel_id=1, source_target_pairs={{0,96},{96,0},{160,64},{192,32},{224,128},{1,97},{97,1},{161,65},{... | collective-permute-start | bytes 393224 | tf_op jit(solution)/shard_map/ppermute | solution.py:344
  73.0 9.1 %collective-permute-start.16 = (bf16[256,256]{1,0:T(8,128)(2,1)S(1)}, bf16[256,256]{1,0:T(8,128)(2,1)S(1)}, u32[]{:S(2)}, u32[]{:S(2)}) collective-permute-start(bf16[256,256]{1,0:T(8,128)(2,1)S(1)} %get-tuple-element.41), channel_id=1, source_target_pairs={{0,32},{192,0},{224,64},{1,33},{193,1},{225,65},{2,34},{194,2},{22... | collective-permute-start | bytes 393224 | tf_op jit(solution)/shard_map/ppermute | solution.py:344
  75.1 8.6 %collective-permute-start.13 = (bf16[128,512]{1,0:T(8,128)(2,1)S(1)}, bf16[128,512]{1,0:T(8,128)(2,1)S(1)}, u32[]{:S(2)}, u32[]{:S(2)}) collective-permute-start(bf16[128,512]{1,0:T(8,128)(2,1)S(1)} %pad_maximum_fusion), channel_id=1, source_target_pairs={{0,224},{32,64},{64,32},{96,128},{128,96},{160,192},{192,160},{224... | collective-permute-start | bytes 393224 | tf_op jit(solution)/shard_map/ppermute | solution.py:255
